TPU v7x, 256 devices: a whole 4x4x8 slice. The times are simulated.
256 devices in a mesh: ep: 16 (over y, z_lo, core), etp: 16 (over z_hi, x).
Axes of the slice: x: 4, y: 4, z: 8 (z_hi: 4, z_lo: 2; z = z_hi * 2 + z_lo), core: 2. Of those that a mesh axis runs over, the one named last changes fastest.
Arguments:
- tokens: bfloat16 [32768, 7168], P(('ep', 'etp')), may hold values from -6 to 6
- expert_ids: int32 [32768, 8], P(('ep', 'etp')), may hold values from 0 to 383, all different within a row; in each aligned block of 128 rows (0 to 127, 128 to 255, ...) at most 3 rows name the same one
- gate_q: int32 [32768, 8], P(('ep', 'etp')), may hold values from 1 to 1024
- w_gate: bfloat16 [16, 7168, 2048], P('ep', None, 'etp'), may hold values from -0.0625 to 0.0625
- w_up: bfloat16 [16, 7168, 2048], P('ep', None, 'etp'), may hold values from -0.0625 to 0.0625
- w_down: bfloat16 [16, 2048, 7168], P('ep', 'etp'), may hold values from -0.125 to 0.125
Outputs:
- mixed: bfloat16 [32768, 7168], P(('ep', 'etp'))
Inputs may be any that keep to these rules, and one draw needn't show every extreme that they name: `expert_ids`: each row names 8 different experts; among the 128 rows of one device no expert is named by more than 3 rows.
All inputs are finite; a program needn't handle non-finite values.
Results may differ from a plain program's by a relative error of at most 0.014.
Values may be sent and summed in bfloat16 or wider, within the bound.
A program may use at most 64 MiB of HBM per device.

v0:
```python
import jax
import jax.numpy as jnp
from jax import lax
from jax.sharding import PartitionSpec as P

CAP = 3


def laid_out(blocks, dim):
    dims = list(blocks.shape[1:])
    dims[dim] *= blocks.shape[0]
    return jnp.moveaxis(blocks, 0, dim).reshape(dims)


def work_in_pieces(x, axis, dim, work, out_dim):
    span = x.shape[dim]
    pieces = jnp.split(x, 2, axis=dim) if span % 2 == 0 else [x]
    first = jnp.arange(lax.axis_size(axis)) * span
    blocks = [lax.all_gather(slab, axis) for slab in pieces]
    made = [jax.vmap(work)(b, first + k * (span // len(pieces))) for k, b in enumerate(blocks)]
    return laid_out(jnp.concatenate(made, axis=out_dim + 1), out_dim)


def body(tokens, expert_ids, gate_q, w_gate, w_up, w_down):
    groups = lax.axis_size("ep")
    members = lax.axis_size("etp")
    capacity = CAP
    width = tokens.shape[1]
    count_rows = tokens.shape[0]
    flat_ids = expert_ids.reshape(-1)
    owner_hot = (flat_ids[:, None] == jnp.arange(groups, dtype=jnp.int32)[None, :]).astype(
        jnp.int32
    )
    earlier = jnp.cumsum(owner_hot, axis=0) - owner_hot
    position = jnp.sum(earlier * owner_hot, axis=1)
    column = jnp.where(flat_ids < groups, flat_ids * capacity + position, -1)
    select = (column[:, None] == jnp.arange(groups * capacity, dtype=jnp.int32)[None, :]).astype(
        jnp.float32
    )
    select = select.reshape(count_rows, -1, groups * capacity)
    placing = jnp.sum(select, axis=1)
    gate_scale = gate_q.astype(jnp.float32) / 1024.0
    scaling = jnp.sum(select * gate_scale[:, :, None], axis=1)
    bucket = jnp.einsum(
        "tc,td->cd", placing.astype(jnp.bfloat16), tokens, preferred_element_type=jnp.float32
    )
    bucket = bucket.astype(jnp.bfloat16).reshape(groups, capacity, width)

    def expert_hidden(arrived):
        gate = jnp.dot(arrived, w_gate[0], preferred_element_type=jnp.float32)
        upper = jnp.dot(arrived, w_up[0], preferred_element_type=jnp.float32)
        return (jax.nn.silu(gate) * upper).astype(jnp.bfloat16)

    arrived = lax.all_to_all(bucket, "ep", split_axis=0, concat_axis=0, tiled=True)

    def hidden_piece(piece, start):
        return expert_hidden(piece)

    hidden = work_in_pieces(arrived, "etp", 1, hidden_piece, 1)
    inner = hidden.shape[2]
    ordered = (
        hidden.reshape(groups, members, capacity, inner).transpose(1, 0, 2, 3).reshape(-1, inner)
    )
    piece = ordered
    term = jnp.dot(piece, w_down[0], preferred_element_type=jnp.float32)
    rounded = lax.optimization_barrier(term.astype(jnp.bfloat16))
    summed = lax.psum_scatter(
        rounded.astype(jnp.float32).astype(jnp.bfloat16), "etp", scatter_dimension=0, tiled=True
    )
    local_out = summed.reshape(groups, capacity, width)
    results = lax.all_to_all(local_out, "ep", split_axis=0, concat_axis=0, tiled=True)
    flat_out = results.reshape(groups * capacity, width).astype(jnp.float32)
    mixed = jnp.dot(scaling, flat_out)
    return mixed.astype(jnp.bfloat16)


def solution(mesh):
    in_specs = (
        P(("ep", "etp"), None),
        P(("ep", "etp"), None),
        P(("ep", "etp"), None),
        P("ep", None, "etp"),
        P("ep", None, "etp"),
        P("ep", "etp", None),
    )
    out_specs = P(("ep", "etp"), None)
    return jax.shard_map(body, mesh=mesh, in_specs=in_specs, out_specs=out_specs, check_vma=False)
```

profile of v0, /device:TPU:1, one launch (start us, length us, event | category | flops | bytes accessed | tf_op | source)
XLA Modules:
  0.0 373.8 jit_solution(3574039436163450649)
XLA Ops:
  6.5 0.0 copy-start
  6.5 0.0 all-gather.3.cloned.1.call-start
  6.5 0.9 copy.50
  7.5 0.1 eq.43
  7.6 0.1 eq.39
  7.6 0.7 convert_multiply_fusion
  8.3 4.5 %reduce-window.6 = s32[16,8,128]{2,1,0:T(8,128)S(1)} reduce-window(s32[16,8,128]{2,1,0:T(8,128)S(1)} %fusion.20, s32[]{:T(128)} %constant.16.clone.1), window={size=1x1x128 pad=0_0x0_0x127_0}, to_apply=%region_0.0 | reduce-window | flops 2080768 | bytes 131076 | tf_op jit(solution)/shard_map/reduce-window
  12.9 0.1 slice.8
  12.9 0.1 copy.52
  13.1 0.1 copy.53
  13.2 0.1 broadcast_add_fusion
  13.3 0.1 reduce_sum.30
  13.5 0.7 add_select_fusion
  14.2 1.9 convolution_convert_fusion.2
  16.1 0.4 reshape.53
  16.6 21.0 %all_to_all.10 = bf16[16,3,7168]{2,1,0:T(4,128)(2,1)S(1)} all-to-all(bf16[16,3,7168]{2,1,0:T(4,128)(2,1)S(1)} %reshape.53), channel_id=1, replica_groups=mesh['ep'=16,'etp'=16] {'ep'}, dimensions={0} | all-to-all | bytes 1376256 | tf_op jit(solution)/shard_map/all_to_all | solution.py:54
  37.6 1.1 copy.55
  38.7 0.0 all-gather.3.cloned.1.call-update
  38.7 0.0 reduce-scatter.2.cloned.1.call-start
  38.7 132.3 %all-gather.3.cloned.1.call-done = bf16[256,3,7168]{2,0,1:T(8,128)(2,1)} async-done(((bf16[16,3,7168]{2,0,1:T(8,128)(2,1)}), bf16[256,3,7168]{2,0,1:T(8,128)(2,1)}) %all-gather.3.cloned.1.call-update) | async-done | bytes 11010064 | tf_op jit(solution)/shard_map/all_gather | solution.py:19
  171.0 0.0 copy-start.1
  171.0 0.0 copy-start.2
  171.0 6.5 %fusion.2 = f32[16,16,3,128]{3,1,2,0:T(8,128)S(1)} fusion(bf16[16,16,3,7168]{3,1,0,2:T(8,128)(2,1)} %bitcast.47, bf16[1,7168,128]{2,1,0:T(8,128)(2,1)} %param.9), kind=kOutput, calls=%fused_computation.3 | convolution fusion | flops 1409286144 | bytes 13238272 | tf_op jit(solution)/shard_map/vmap()/dot_general | solution.py:50
  177.5 1.4 copy-done.1
  178.9 0.5 copy-done.2
  179.4 3.0 fusion.12
  182.4 0.1 copy.58
  182.5 0.2 reshape.54
  182.6 0.0 copy-done
  182.7 5.7 %convolution_convert_fusion = bf16[768,7168]{1,0:T(8,128)(2,1)} fusion(bf16[768,128]{1,0:T(8,128)(2,1)S(1)} %reshape.54, bf16[1,128,7168]{2,1,0:T(8,128)(2,1)S(1)} %copy-done), kind=kOutput, calls=%fused_computation | convolution fusion | flops 1414791168 | bytes 13041664 | tf_op jit(solution)/shard_map/dot_general | solution.py:65
  188.4 0.0 reduce-scatter.2.cloned.1.call-update
  188.4 154.7 %reduce-scatter.2.cloned.1.call-done = bf16[48,7168]{1,0:T(8,128)(2,1)} async-done(((bf16[768,7168]{1,0:T(8,128)(2,1)}), bf16[48,7168]{1,0:T(8,128)(2,1)}) %reduce-scatter.2.cloned.1.call-update) | async-done | bytes 688144 | tf_op jit(solution)/shard_map/reduce_scatter | solution.py:67
  343.2 1.4 reshape.55
  344.6 18.8 %all_to_all.11 = bf16[16,3,7168]{2,1,0:T(4,128)(2,1)} all-to-all(bf16[16,3,7168]{2,1,0:T(4,128)(2,1)S(1)} %reshape.55), channel_id=1, replica_groups=mesh['ep'=16,'etp'=16] {'ep'}, dimensions={0} | all-to-all | bytes 1376256 | tf_op jit(solution)/shard_map/all_to_all | solution.py:71
  363.4 1.6 reshape.56
  365.0 1.9 fusion.22
  (6 shorter events, 0.2 us)
Async XLA Ops:
  6.5 176.1 %copy-start = (bf16[1,128,7168]{2,1,0:T(8,128)(2,1)S(1)}, bf16[1,128,7168]{2,1,0:T(8,128)(2,1)}, u32[]{:S(2)}) copy-start(bf16[1,128,7168]{2,1,0:T(8,128)(2,1)} %param.11) | copy-start | bytes 5505028
  6.5 164.5 %all-gather.3.cloned.1.call-start = ((), (), s32[]{:S(2)}) async-start(), calls=%async_computation.4 | async-start | bytes 11698176 | tf_op jit(solution)/shard_map/all_gather | solution.py:19
  38.7 304.5 %reduce-scatter.2.cloned.1.call-start = ((), (), s32[]{:S(2)}) async-start(), calls=%async_computation.3 | async-start | bytes 11698176 | tf_op jit(solution)/shard_map/reduce_scatter | solution.py:67
  171.0 7.8 %copy-start.1 = (bf16[256,3,7168]{2,0,1:T(8,128)(2,1)S(1)}, bf16[256,3,7168]{2,0,1:T(8,128)(2,1)}, u32[]{:S(2)}) copy-start(bf16[256,3,7168]{2,0,1:T(8,128)(2,1)} %all-gather.3.cloned.1.call-done) | copy-start | bytes 33030148
  171.0 8.3 %copy-start.2 = (bf16[1,7168,128]{2,1,0:T(8,128)(2,1)S(1)}, bf16[1,7168,128]{2,1,0:T(8,128)(2,1)}, u32[]{:S(2)}) copy-start(bf16[1,7168,128]{2,1,0:T(8,128)(2,1)} %param.10) | copy-start | bytes 5505028
Sparse Core Ops, SparseCore 0:
  38.8 132.1 all-gather.2
  188.5 154.5 reduce-scatter.1
where the time goes:
time: 374 us
  waiting for transfers between devices  287 us (77%)
  blocking collectives  39.8 us (11%)
  matrix products  19 us (5%)
  between operations  13.5 us (4%)
  local copies, waits for them, and re-layouts  8.25 us (2%)
  other arithmetic  6.12 us (2%)
    reduce_scatter x1, waiting for transfers between devices, body(): lax.psum_scatter(rounded.astype(jnp.float32).astype(jnp.bfloat16), 'etp',...  155 us
    all_gather x1, waiting for transfers between devices, work_in_pieces(): blocks = [lax.all_gather(slab, axis) for slab in pieces]  132 us
    all_to_all x1, blocking collectives, body(): lax.all_to_all(bucket, 'ep', split_axis=0, concat_axis=0, tiled=True)  21 us
    all_to_all x1, blocking collectives, body(): lax.all_to_all(local_out, 'ep', split_axis=0, concat_axis=0, tiled=True)  18.8 us
  transfers between devices with their start and end apart: 2, of which 2 were waited for; matrix products, arithmetic and copies ran while one was open for 0% of the time, Pallas kernels for 0%

commit v1 on v0

v1 whole, which is shorter than its diff:
```python
import functools

import jax
import jax.numpy as jnp
import numpy as np
from jax import lax
from jax.experimental import pallas as pl
from jax.experimental.pallas import tpu as pltpu
from jax.sharding import PartitionSpec as P

CAP = 3
RING = 4
MESH = pl.DeviceIdType.MESH
F32 = jnp.float32
BF16 = jnp.bfloat16


def third(c):
    return lax.shift_right_logical(c * 43691, 17)


def kernel(ids_ref, gate_ref, p1_ref, p1t_ref, p2_ref, p2t_ref, tok_hbm, wg_hbm, wu_hbm, wd_hbm,
           ret_ref, scal_ref,
           tok, bs, xa, sb, rb, X, wgu, wd, gp, own, hr, H, pown, pfar, pnear, pcomb, rfar, rdir, rcomb,
           sr, rr, ts,
           loc_sem, w_send, w_recv, a_send, a_recv, b_send, b_recv, z_send, z_recv, g_send, g_recv,
           h_send, h_recv, r_send, r_recv, c_send, c_recv, d_send, d_recv):
    ep = lax.axis_index("ep")
    etp = lax.axis_index("etp")
    n_ep = lax.axis_size("ep")
    zi = etp // RING
    x = etp % RING
    width = tok.shape[1]
    D4 = width // RING
    slots = n_ep * CAP
    R = slots * RING
    half = R // 2
    inner = wd.shape[0] // RING

    def xdev(k):
        return (ep, zi * RING + lax.rem(x + k, RING))

    def zdev(k):
        return (ep, lax.rem(zi + k, RING) * RING + x)

    def edev(k):
        return (lax.rem(ep + k, n_ep), etp)

    def send(src, dst, ssem, rsem, dev):
        c = pltpu.make_async_remote_copy(src_ref=src, dst_ref=dst, send_sem=ssem, recv_sem=rsem,
                                         device_id=dev, device_id_type=MESH)
        c.start()
        return c

    def rows(start, size):
        return pl.ds(pl.multiple_of(start, 16), size)

    def cols(start, size):
        return pl.ds(pl.multiple_of(start, 128), size)

    tok_copy = pltpu.make_async_copy(tok_hbm, tok, loc_sem.at[0])
    tok_copy.start()
    w_loc = [
        pltpu.make_async_copy(wg_hbm.at[0, rows(x * D4, D4), :], wgu.at[x, :, pl.ds(0, inner)], loc_sem.at[1]),
        pltpu.make_async_copy(wu_hbm.at[0, rows(x * D4, D4), :], wgu.at[x, :, pl.ds(inner, inner)], loc_sem.at[2]),
        pltpu.make_async_copy(wd_hbm.at[0, :, cols(x * D4, D4)], wd.at[rows(x * inner, inner), :], loc_sem.at[3]),
    ]

    barrier = pltpu.get_barrier_semaphore()
    for k in range(1, RING):
        pl.semaphore_signal(barrier, inc=1, device_id=xdev(k), device_id_type=MESH)
    for k in (1, RING - 1):
        pl.semaphore_signal(barrier, inc=1, device_id=zdev(k), device_id_type=MESH)
    for k in range(1, n_ep):
        pl.semaphore_signal(barrier, inc=1, device_id=edev(k), device_id_type=MESH)

    T = tok.shape[0]
    c = lax.broadcasted_iota(jnp.int32, (slots, T), 0)
    expert = third(c)
    slot = (c - CAP * expert).astype(F32)
    hot = jnp.zeros((slots, T), F32)
    weight = jnp.zeros((slots, T), F32)
    for r in range(ids_ref.shape[0]):
        eq = ids_ref[r:r + 1, :] == expert
        hot = jnp.where(eq, 1.0, hot)
        weight = jnp.where(eq, gate_ref[r:r + 1, :].astype(F32), weight)
    before = lax.broadcasted_iota(jnp.int32, (T, T), 0) < lax.broadcasted_iota(jnp.int32, (T, T), 1)
    earlier = jnp.dot(hot.astype(BF16), jnp.where(before, 1.0, 0.0).astype(BF16), preferred_element_type=F32)
    placing = jnp.where(earlier == slot, hot, 0.0)
    scal_ref[...] = placing * weight * (1.0 / 1024.0)
    placing = placing.astype(BF16)

    tok_copy.wait()
    pl.semaphore_wait(barrier, (RING - 1) + 2 + (n_ep - 1))

    a_copies = []
    for k in (2, 1, 3, 0):
        dst_x = lax.rem(x + k, RING)
        piece = jnp.dot(placing, tok[:, cols(dst_x * D4, D4)], preferred_element_type=F32).astype(BF16)
        if k == 0:
            xa[rows(x * slots, slots), :] = piece
        else:
            bs[k - 1] = piece
            a_copies.append(send(bs.at[k - 1], xa.at[rows(x * slots, slots), :], a_send.at[k - 1], a_recv.at[k - 1], xdev(k)))

    w_copies = []
    for i, k in enumerate((1, 3, 2)):
        dst_x = lax.rem(x + k, RING)
        w_copies.append(send(wg_hbm.at[0, rows(dst_x * D4, D4), :], wgu.at[x, :, pl.ds(0, inner)],
                             w_send.at[0, i], w_recv.at[0, i], xdev(k)))
        w_copies.append(send(wu_hbm.at[0, rows(dst_x * D4, D4), :], wgu.at[x, :, pl.ds(inner, inner)],
                             w_send.at[1, i], w_recv.at[1, i], xdev(k)))
    d_copies = []
    for i, k in enumerate((1, 3, 2)):
        dst_x = lax.rem(x + k, RING)
        d_copies.append(send(wd_hbm.at[0, :, cols(dst_x * D4, D4)], wd.at[rows(x * inner, inner), :],
                             w_send.at[2, i], w_recv.at[2, i], xdev(k)))
    for cp in w_loc:
        cp.start()

    for cp in a_copies:
        cp.wait_recv()

    sb[...] = jnp.dot(p1_ref[...], xa[...], preferred_element_type=F32).astype(BF16)
    b_copies = []
    for k in range(1, n_ep):
        dst_e = lax.rem(ep + k, n_ep)
        b_copies.append(send(sb.at[rows(dst_e * 16, 16), :], rb.at[rows(ep * 16, 16), :],
                             b_send.at[k - 1], b_recv.at[k - 1], edev(k)))
    rb[rows(ep * 16, 16), :] = sb[rows(ep * 16, 16), :]
    for cp in b_copies:
        cp.wait_recv()
    X[rows(zi * R, R), :] = jnp.dot(p2_ref[...], rb[...], preferred_element_type=F32).astype(BF16)

    zm = lax.rem(zi + RING - 1, RING)
    zp = lax.rem(zi + 1, RING)
    zf = lax.rem(zi + 2, RING)

    def zsend(block, lo, i, k):
        part = X.at[rows(block * R + (0 if lo else half), half), :]
        return send(part, part, z_send.at[i], z_recv.at[i], zdev(k))

    zc = [None] * 6
    zc[0] = zsend(zi, True, 0, 1)
    zc[3] = zsend(zi, False, 3, RING - 1)
    zc[1] = zsend(zi, False, 1, 1)
    zc[4] = zsend(zi, True, 4, RING - 1)
    zc[0].wait_recv()
    zc[2] = zsend(zm, True, 2, 1)
    zc[3].wait_recv()
    zc[5] = zsend(zp, False, 5, RING - 1)

    for cp in w_copies:
        cp.wait_recv()
    w_loc[0].wait()
    w_loc[1].wait()

    order = [zi, zm, zp, zf]
    g_copies = [[None] * (RING - 1) for _ in range(4)]
    h_copies = [[None] * (RING - 1) for _ in range(4)]

    def first(i):
        b = order[i]
        xs = X[rows(b * R, R), :]
        for k in (2, 1, 3, 0):
            dst_x = lax.rem(x + k, RING)
            acc = jnp.dot(xs, wgu[dst_x], preferred_element_type=F32)
            if k == 0:
                own[i] = acc
            else:
                gp[i, k - 1] = acc.astype(BF16)
                g_copies[i][k - 1] = send(gp.at[i, k - 1], hr.at[i, k - 1], g_send.at[i, k - 1],
                                          g_recv.at[i, k - 1], xdev(k))

    def second(i):
        b = order[i]
        total = own[i]
        for k in range(RING - 1):
            g_copies[i][k].wait_recv()
            total = total + hr[i, k].astype(F32)
        g = total[:, :inner]
        u = total[:, inner:]
        H[rows(b * R, R), cols(x * inner, inner)] = (g / (1.0 + jnp.exp(-g)) * u).astype(BF16)
        for k in range(1, RING):
            part = H.at[rows(b * R, R), cols(x * inner, inner)]
            h_copies[i][k - 1] = send(part, part, h_send.at[i, k - 1], h_recv.at[i, k - 1], xdev(k))

    def third_(i):
        b = order[i]
        for k in range(RING - 1):
            h_copies[i][k].wait_recv()
        return jnp.dot(H[rows(b * R, R), :], wd[...], preferred_element_type=F32)

    first(0)
    zc[1].wait_recv()
    first(1)
    zc[4].wait_recv()
    first(2)
    second(0)
    second(1)
    zc[2].wait_recv()
    zc[5].wait_recv()
    first(3)
    second(2)
    second(3)
    for cp in d_copies:
        cp.wait_recv()
    w_loc[2].wait()

    def rsend(src, dst, i, k):
        return send(src, dst, r_send.at[i], r_recv.at[i], zdev(k))

    lo, hi = slice(0, half), slice(half, R)
    rc = [None] * 6
    far = third_(3)
    pfar[...] = far.astype(BF16)
    rc[0] = rsend(pfar.at[pl.ds(0, half), :], rfar.at[0], 0, 1)
    rc[3] = rsend(pfar.at[pl.ds(half, half), :], rfar.at[1], 3, RING - 1)
    up = third_(2)
    pnear[0] = up[hi].astype(BF16)
    pcomb[0] = up[lo].astype(BF16)
    rc[1] = rsend(pnear.at[0], rdir.at[0], 1, 1)
    down = third_(1)
    pnear[1] = down[lo].astype(BF16)
    pcomb[1] = down[hi].astype(BF16)
    rc[4] = rsend(pnear.at[1], rdir.at[1], 4, RING - 1)
    pown[...] = third_(0)
    rc[0].wait_recv()
    pcomb[0] = (pcomb[0].astype(F32) + rfar[0].astype(F32)).astype(BF16)
    rc[2] = rsend(pcomb.at[0], rcomb.at[0], 2, 1)
    rc[3].wait_recv()
    pcomb[1] = (pcomb[1].astype(F32) + rfar[1].astype(F32)).astype(BF16)
    rc[5] = rsend(pcomb.at[1], rcomb.at[1], 5, RING - 1)
    rc[1].wait_recv()
    rc[4].wait_recv()
    rc[2].wait_recv()
    rc[5].wait_recv()
    y_lo = pown[pl.ds(0, half), :] + rcomb[0].astype(F32) + rdir[1].astype(F32)
    y_hi = pown[pl.ds(half, half), :] + rcomb[1].astype(F32) + rdir[0].astype(F32)
    y = jnp.concatenate([y_lo.astype(BF16), y_hi.astype(BF16)], axis=0)

    sr[...] = jnp.dot(p2t_ref[...], y, preferred_element_type=F32).astype(BF16)
    cc = []
    for k in range(1, n_ep):
        dst_e = lax.rem(ep + k, n_ep)
        cc.append(send(sr.at[rows(dst_e * 16, 16), :], rr.at[rows(ep * 16, 16), :],
                       c_send.at[k - 1], c_recv.at[k - 1], edev(k)))
    rr[rows(ep * 16, 16), :] = sr[rows(ep * 16, 16), :]
    for cp in cc:
        cp.wait_recv()
    ts[...] = jnp.dot(p1t_ref[...], rr[...], preferred_element_type=F32).astype(BF16)
    dc = []
    for k in range(1, RING):
        dst_x = lax.rem(x + k, RING)
        dc.append(send(ts.at[rows(dst_x * slots, slots), :], ret_ref.at[:, cols(x * D4, D4)],
                       d_send.at[k - 1], d_recv.at[k - 1], xdev(k)))
    ret_ref[:, cols(x * D4, D4)] = ts[rows(x * slots, slots), :]
    for cp in dc:
        cp.wait_recv()
    for group in [a_copies, w_copies, d_copies, b_copies, zc, rc, cc, dc] + g_copies + h_copies:
        for cp in group:
            cp.wait_send()


def body(tokens, expert_ids, gate_q, w_gate, w_up, w_down):
    n_ep = lax.axis_size("ep")
    T, width = tokens.shape
    D4 = width // RING
    slots = n_ep * CAP
    R = slots * RING
    inner = w_down.shape[1]
    per = CAP * RING

    p1 = np.zeros((n_ep * 16, R), np.float32)
    p2 = np.zeros((R, n_ep * 16), np.float32)
    for e in range(n_ep):
        for s in range(RING):
            for q in range(CAP):
                p1[e * 16 + s * CAP + q, s * slots + e * CAP + q] = 1
        for j in range(per):
            p2[e * per + j, e * 16 + j] = 1
    consts = [jnp.asarray(m, BF16) for m in (p1, p1.T, p2, p2.T)]

    vm = pl.BlockSpec(memory_space=pltpu.VMEM)
    anyspec = pl.BlockSpec(memory_space=pl.ANY)
    V = pltpu.VMEM
    DMA = pltpu.SemaphoreType.DMA
    half = R // 2
    scratch = [
        V((T, width), BF16),
        V((3, slots, D4), BF16),
        V((R, D4), BF16),
        V((n_ep * 16, D4), BF16),
        V((n_ep * 16, D4), BF16),
        V((RING * R, D4), BF16),
        V((RING, D4, 2 * inner), BF16),
        V((RING * inner, D4), BF16),
        V((RING, 3, R, 2 * inner), BF16),
        V((RING, R, 2 * inner), F32),
        V((RING, 3, R, 2 * inner), BF16),
        V((RING * R, RING * inner), BF16),
        V((R, D4), F32),
        V((R, D4), BF16),
        V((2, half, D4), BF16),
        V((2, half, D4), BF16),
        V((2, half, D4), BF16),
        V((2, half, D4), BF16),
        V((2, half, D4), BF16),
        V((n_ep * 16, D4), BF16),
        V((n_ep * 16, D4), BF16),
        V((R, D4), BF16),
        DMA((4,)), DMA((3, 3)), DMA((3, 3)), DMA((3,)), DMA((3,)),
        DMA((n_ep - 1,)), DMA((n_ep - 1,)), DMA((6,)), DMA((6,)),
        DMA((4, 3)), DMA((4, 3)), DMA((4, 3)), DMA((4, 3)), DMA((6,)), DMA((6,)),
        DMA((n_ep - 1,)), DMA((n_ep - 1,)), DMA((3,)), DMA((3,)),
    ]
    ret, scal = pl.pallas_call(
        kernel,
        out_shape=(jax.ShapeDtypeStruct((slots, width), BF16), jax.ShapeDtypeStruct((slots, T), F32)),
        in_specs=[vm] * 6 + [anyspec] * 4,
        out_specs=(vm, vm),
        scratch_shapes=scratch,
        compiler_params=pltpu.CompilerParams(collective_id=0, has_side_effects=True, vmem_limit_bytes=60 * 1024 * 1024),
        name="experts",
    )(expert_ids.T, gate_q.T, *consts, tokens, w_gate, w_up, w_down)
    mixed = lax.dot_general(scal, ret.astype(F32), (((0,), (0,)), ((), ())))
    return mixed.astype(BF16)


def solution(mesh):
    in_specs = (
        P(("ep", "etp"), None),
        P(("ep", "etp"), None),
        P(("ep", "etp"), None),
        P("ep", None, "etp"),
        P("ep", None, "etp"),
        P("ep", "etp", None),
    )
    out_specs = P(("ep", "etp"), None)
    return jax.shard_map(body, mesh=mesh, in_specs=in_specs, out_specs=out_specs, check_vma=False)
```

time: 374 us -> 181 us (0.48)
  waiting for transfers between devices: 287 us -> 0 us
  Pallas kernels: 0 us -> 178 us
  blocking collectives: 39.8 us -> 0 us
  matrix products: 19 us -> 3.01 us
  between operations: 13.5 us -> 0.01 us
  local copies, waits for them, and re-layouts: 8.25 us -> 0 us
  other arithmetic: 6.12 us -> 0 us
    pallas_call x0 -> x1, Pallas kernels: none -> 178 us  [body(): pl.pallas_call(kernel, out_shape=(jax.ShapeDtypeStruct((slots, width), BF...]
    reduce_scatter x1 -> x0, waiting for transfers between devices: 155 us -> none  [body(): lax.psum_scatter(rounded.astype(jnp.float32).astype(jnp.bfloat16), 'etp',...]
    all_gather x1 -> x0, waiting for transfers between devices: 132 us -> none  [work_in_pieces(): blocks = [lax.all_gather(slab, axis) for slab in pieces]]
    all_to_all x2 -> x0, blocking collectives: 39.8 us -> none  [the longest x1 21 us: body(): lax.all_to_all(bucket, 'ep', split_axis=0, concat_axis=0, tiled=True)]
    dot_general x5 -> x1, matrix products: 19 us -> 3.01 us  [body(): mixed = lax.dot_general(scal, ret.astype(F32), (((0,), (0,)), ((), ())))]
    another operation x3 -> x0, other arithmetic: 4.64 us -> none
  transfers between devices with their start and end apart: 2 -> 0, of which waited for: 2 -> 0; matrix products, arithmetic and copies ran while one was open for 0% -> 0% of each run, Pallas kernels for 0% -> 0%
where the time goes in v1:
time: 181 us
  Pallas kernels  178 us (98%)
  matrix products  3.01 us (2%)
    pallas_call x1, Pallas kernels, body(): pl.pallas_call(kernel, out_shape=(jax.ShapeDtypeStruct((slots, width), BF...  178 us

profile of v1, /device:TPU:1, one launch (start us, length us, event | category | flops | bytes accessed | tf_op | source)
XLA Modules:
  0.0 181.1 jit_solution(11947225932299965481)
XLA Ops:
  0.0 178.1 %experts.1 = (bf16[48,7168]{1,0:T(8,128)(2,1)}, f32[48,128]{1,0:T(8,128)}) custom-call(s32[8,128]{1,0:T(8,128)} %bitcast.4, s32[8,128]{1,0:T(8,128)} %bitcast.5, bf16[256,192]{1,0:T(8,128)(2,1)} %constant.8.clone.p1_ref, bf16[192,256]{1,0:T(8,128)(2,1)} %constant.9.clone.p1t_ref, bf16[192,256]{1,0:T(8,128)(2,1)} %constant.10.clone.p2_ref, ...), custom_call_target="tpu_custom_call" | custom-call | tf_op jit(solution)/shard_map/experts/pallas_call | solution.py:317
  178.1 3.0 %fusion = bf16[128,7168]{1,0:T(8,128)(2,1)} fusion(f32[48,128]{1,0:T(8,128)} %get-tuple-element.7, bf16[48,7168]{1,0:T(8,128)(2,1)} %get-tuple-element.8), kind=kOutput, calls=%fused_computation.1 | convolution fusion | flops 88080384 | bytes 2547712 | tf_op jit(solution)/shard_map/dot_general | solution.py:326

commit v2 on v1

v2 whole, which is shorter than its diff:
```python
import jax
import jax.numpy as jnp
import numpy as np
from jax import lax
from jax.experimental import pallas as pl
from jax.experimental.pallas import tpu as pltpu
from jax.sharding import PartitionSpec as P

CAP = 3
RING = 4
C = 2
MESH = pl.DeviceIdType.MESH
F32 = jnp.float32
BF16 = jnp.bfloat16
scope = jax.named_scope


def third(c):
    return lax.shift_right_logical(c * 43691, 17)


def dot(a, b):
    return jnp.dot(a, b, preferred_element_type=F32)


def kernel(ids_ref, gate_ref, p1_ref, p1t_ref, p2_ref, p2t_ref, tok_hbm, wg_hbm, wu_hbm, wd_hbm,
           ret_ref, scal_ref,
           tok, bs, xa, sb, rb, X, wgu, wd, gp, own, hr, H, pown, pfar, pnear, pcomb, rfar, rdir, rcomb,
           sr, rr, ts,
           loc_sem, w_send, w_recv, a_send, a_recv, b_send, b_recv, z_send, z_recv, g_send, g_recv,
           h_send, h_recv, r_send, r_recv, c_send, c_recv, d_send, d_recv):
    ep = lax.axis_index("ep")
    etp = lax.axis_index("etp")
    n_ep = lax.axis_size("ep")
    zi = etp // RING
    x = etp % RING
    width = tok.shape[1]
    D4 = width // RING
    DC = D4 // C
    slots = n_ep * CAP
    R = slots * RING
    half = R // 2
    inner = wd.shape[1] // RING

    def xdev(k):
        return (ep, zi * RING + lax.rem(x + k, RING))

    def zdev(k):
        return (ep, lax.rem(zi + k, RING) * RING + x)

    def edev(k):
        return (lax.rem(ep + k, n_ep), etp)

    everything = []

    def send(src, dst, ssem, rsem, dev):
        c = pltpu.make_async_remote_copy(src_ref=src, dst_ref=dst, send_sem=ssem, recv_sem=rsem,
                                         device_id=dev, device_id_type=MESH)
        c.start()
        everything.append(c)
        return c

    def rows(start, size):
        return pl.ds(pl.multiple_of(start, 16), size)

    def cols(start, size):
        return pl.ds(pl.multiple_of(start, 128), size)

    tok_copy = pltpu.make_async_copy(tok_hbm, tok, loc_sem.at[0])
    tok_copy.start()
    w_loc = [
        pltpu.make_async_copy(wg_hbm.at[0, rows(x * D4, D4), :], wgu.at[x, :, pl.ds(0, inner)], loc_sem.at[1]),
        pltpu.make_async_copy(wu_hbm.at[0, rows(x * D4, D4), :], wgu.at[x, :, pl.ds(inner, inner)], loc_sem.at[2]),
    ] + [
        pltpu.make_async_copy(wd_hbm.at[0, :, cols(x * D4 + q * DC, DC)], wd.at[q, rows(x * inner, inner), :], loc_sem.at[3 + q])
        for q in range(C)
    ]

    barrier = pltpu.get_barrier_semaphore()
    for k in range(1, RING):
        pl.semaphore_signal(barrier, inc=1, device_id=xdev(k), device_id_type=MESH)
    for k in (1, RING - 1):
        pl.semaphore_signal(barrier, inc=1, device_id=zdev(k), device_id_type=MESH)
    for k in range(1, n_ep):
        pl.semaphore_signal(barrier, inc=1, device_id=edev(k), device_id_type=MESH)

    T = tok.shape[0]
    c = lax.broadcasted_iota(jnp.int32, (slots, T), 0)
    expert = third(c)
    slot = (c - CAP * expert).astype(F32)
    hot = jnp.zeros((slots, T), F32)
    weight = jnp.zeros((slots, T), F32)
    for r in range(ids_ref.shape[0]):
        eq = ids_ref[r:r + 1, :] == expert
        hot = jnp.where(eq, 1.0, hot)
        weight = jnp.where(eq, gate_ref[r:r + 1, :].astype(F32), weight)
    before = lax.broadcasted_iota(jnp.int32, (T, T), 0) < lax.broadcasted_iota(jnp.int32, (T, T), 1)
    earlier = dot(hot.astype(BF16), jnp.where(before, 1.0, 0.0).astype(BF16))
    placing = jnp.where(earlier == slot, hot, 0.0)
    scal_ref[...] = placing * weight * (1.0 / 1024.0)
    placing = placing.astype(BF16)

    with scope("tokwait"):
        tok_copy.wait()
    with scope("barrier_in"):
        pl.semaphore_wait(barrier, (RING - 1) + 2 + (n_ep - 1))

    a_copies = [[], []]
    for q in range(C):
        for k in (2, 1, 3, 0):
            dst_x = lax.rem(x + k, RING)
            piece = dot(placing, tok[:, cols(dst_x * D4 + q * DC, DC)]).astype(BF16)
            if k == 0:
                xa[q, rows(x * slots, slots), :] = piece
            else:
                bs[q, k - 1] = piece
                a_copies[q].append(send(bs.at[q, k - 1], xa.at[q, rows(x * slots, slots), :],
                                        a_send.at[q, k - 1], a_recv.at[q, k - 1], xdev(k)))

    w_copies = []
    for i, k in enumerate((1, 3, 2)):
        dst_x = lax.rem(x + k, RING)
        w_copies.append(send(wg_hbm.at[0, rows(dst_x * D4, D4), :], wgu.at[x, :, pl.ds(0, inner)],
                             w_send.at[0, i], w_recv.at[0, i], xdev(k)))
        w_copies.append(send(wu_hbm.at[0, rows(dst_x * D4, D4), :], wgu.at[x, :, pl.ds(inner, inner)],
                             w_send.at[1, i], w_recv.at[1, i], xdev(k)))

    def send_down(q):
        out = []
        for i, k in enumerate((1, 3, 2)):
            dst_x = lax.rem(x + k, RING)
            out.append(send(wd_hbm.at[0, :, cols(dst_x * D4 + q * DC, DC)],
                            wd.at[q, rows(x * inner, inner), :],
                            w_send.at[2 + q, i], w_recv.at[2 + q, i], xdev(k)))
        return out

    d_copies = [send_down(0)]
    for cp in w_loc:
        cp.start()

    b_copies = [[], []]
    for q in range(C):
        with scope("A_wait"):
            for cp in a_copies[q]:
                cp.wait_recv()
        sb[q] = dot(p1_ref[...], xa[q]).astype(BF16)
        for k in range(1, n_ep):
            dst_e = lax.rem(ep + k, n_ep)
            b_copies[q].append(send(sb.at[q, rows(dst_e * 16, 16), :], rb.at[q, rows(ep * 16, 16), :],
                                    b_send.at[q, k - 1], b_recv.at[q, k - 1], edev(k)))
        rb[q, rows(ep * 16, 16), :] = sb[q, rows(ep * 16, 16), :]

    zm = lax.rem(zi + RING - 1, RING)
    zp = lax.rem(zi + 1, RING)
    zf = lax.rem(zi + 2, RING)

    def unit(b, h):
        return rows((2 * b + h) * half, half)

    def zsend(q, b, h, i, k):
        part = X.at[q, unit(b, h), :]
        return send(part, part, z_send.at[q, i], z_recv.at[q, i], zdev(k))

    UP, DOWN = 1, RING - 1
    zc = [[None] * 6 for _ in range(C)]
    for q in range(C):
        with scope("B_wait"):
            for cp in b_copies[q]:
                cp.wait_recv()
        X[q, rows(zi * R, R), :] = dot(p2_ref[...], rb[q]).astype(BF16)
        zc[q][0] = zsend(q, zi, 0, 0, UP)
        zc[q][3] = zsend(q, zi, 1, 3, DOWN)
    for q in range(C):
        with scope("Z0_wait"):
            zc[q][0].wait_recv()
        zc[q][2] = zsend(q, zm, 0, 2, UP)
        with scope("Z3_wait"):
            zc[q][3].wait_recv()
        zc[q][5] = zsend(q, zp, 1, 5, DOWN)
    for q in range(C):
        zc[q][1] = zsend(q, zi, 1, 1, UP)
        zc[q][4] = zsend(q, zi, 0, 4, DOWN)

    with scope("W_wait"):
        for cp in w_copies:
            cp.wait_recv()
        w_loc[0].wait()
        w_loc[1].wait()

    N, F, M, O = range(4)
    pairs = [((zp, 1), (zm, 0)), ((zf, 0), (zf, 1)), ((zp, 0), (zm, 1)), ((zi, 0), (zi, 1))]
    g_copies = [[None] * (RING - 1) for _ in range(4)]
    h_copies = [[None] * (RING - 1) for _ in range(4)]

    def zwait(*which):
        with scope("zwait%d" % which[0]):
            for q in range(C):
                for i in which:
                    zc[q][i].wait_recv()

    def first(i):
        with scope("first%d" % i):
            xs = [jnp.concatenate([X[q, unit(*u), :] for u in pairs[i]], axis=0) for q in range(C)]
            for k in (2, 1, 3, 0):
                dst_x = lax.rem(x + k, RING)
                acc = dot(xs[0], wgu[dst_x, pl.ds(0, DC), :])
                for q in range(1, C):
                    acc = acc + dot(xs[q], wgu[dst_x, pl.ds(q * DC, DC), :])
                if k == 0:
                    own[i] = acc
                else:
                    gp[i, k - 1] = acc.astype(BF16)
                    g_copies[i][k - 1] = send(gp.at[i, k - 1], hr.at[i, k - 1], g_send.at[i, k - 1],
                                              g_recv.at[i, k - 1], xdev(k))

    def second(i):
        with scope("gwait%d" % i):
            for k in range(RING - 1):
                g_copies[i][k].wait_recv()
        with scope("second%d" % i):
            total = own[i]
            for k in range(RING - 1):
                total = total + hr[i, k].astype(F32)
            g = total[:, :inner]
            u = total[:, inner:]
            part = H.at[i, :, cols(x * inner, inner)]
            part[...] = (g / (1.0 + jnp.exp(-g)) * u).astype(BF16)
            for k in (2, 1, 3):
                h_copies[i][k - 1] = send(part, part, h_send.at[i, k - 1], h_recv.at[i, k - 1], xdev(k))

    def hwait(i):
        with scope("hwait%d" % i):
            for k in range(RING - 1):
                h_copies[i][k].wait_recv()

    def dwait(q):
        with scope("dwait%d" % q):
            for cp in d_copies[q]:
                cp.wait_recv()
            w_loc[2 + q].wait()

    def down(i, q):
        return dot(H[i], wd[q])

    rc = [[None] * 6 for _ in range(C)]

    def rsend(buf, into, q, step):
        for j, k in ((0, UP), (1, DOWN)):
            i = step + 3 * j
            rc[q][i] = send(buf.at[q, pl.ds(j * half, half), :], into.at[q, j],
                            r_send.at[q, i], r_recv.at[q, i], zdev(k))

    def near(q):
        with scope("near%d" % q):
            pnear[q] = down(N, q).astype(BF16)

    def far(q):
        with scope("far%d" % q):
            pfar[q] = down(F, q).astype(BF16)
            rsend(pfar, rfar, q, 0)

    def combine(q):
        with scope("comb%d" % q):
            part = down(M, q)
        with scope("S1w%d" % q):
            rc[q][0].wait_recv()
            rc[q][3].wait_recv()
        for j in range(2):
            pcomb[q, pl.ds(j * half, half), :] = (part[j * half:(j + 1) * half] + rfar[q, j].astype(F32)).astype(BF16)
        rsend(pcomb, rcomb, q, 2)

    first(N)
    first(O)
    second(N)
    zwait(2, 5)
    first(F)
    zwait(1, 4)
    first(M)
    hwait(N)
    dwait(0)
    near(0)
    rsend(pnear, rdir, 0, 1)
    second(F)
    d_copies.append(send_down(1))
    second(M)
    second(O)
    hwait(F)
    far(0)
    dwait(1)
    far(1)
    near(1)
    hwait(M)
    combine(0)
    rsend(pnear, rdir, 1, 1)
    combine(1)
    hwait(O)
    with scope("own"):
        for q in range(C):
            pown[q] = down(O, q)

    cc = [[], []]
    for q in range(C):
        with scope("S3w"):
            for i in (1, 4, 2, 5):
                rc[q][i].wait_recv()
        y_lo = pown[q, pl.ds(0, half), :] + rcomb[q, 0].astype(F32) + rdir[q, 1].astype(F32)
        y_hi = pown[q, pl.ds(half, half), :] + rcomb[q, 1].astype(F32) + rdir[q, 0].astype(F32)
        y = jnp.concatenate([y_lo.astype(BF16), y_hi.astype(BF16)], axis=0)
        sr[q] = dot(p2t_ref[...], y).astype(BF16)
        for k in range(1, n_ep):
            dst_e = lax.rem(ep + k, n_ep)
            cc[q].append(send(sr.at[q, rows(dst_e * 16, 16), :], rr.at[q, rows(ep * 16, 16), :],
                              c_send.at[q, k - 1], c_recv.at[q, k - 1], edev(k)))
        rr[q, rows(ep * 16, 16), :] = sr[q, rows(ep * 16, 16), :]
    dc = [[], []]
    for q in range(C):
        with scope("RBw"):
            for cp in cc[q]:
                cp.wait_recv()
        ts[q] = dot(p1t_ref[...], rr[q]).astype(BF16)
        for k in (2, 1, 3):
            dst_x = lax.rem(x + k, RING)
            dc[q].append(send(ts.at[q, rows(dst_x * slots, slots), :], ret_ref.at[:, cols(x * D4 + q * DC, DC)],
                              d_send.at[q, k - 1], d_recv.at[q, k - 1], xdev(k)))
        ret_ref[:, cols(x * D4 + q * DC, DC)] = ts[q, rows(x * slots, slots), :]
    with scope("RAw"):
        for q in range(C):
            for cp in dc[q]:
                cp.wait_recv()
    with scope("sends"):
        for cp in everything:
            cp.wait_send()


def body(tokens, expert_ids, gate_q, w_gate, w_up, w_down):
    n_ep = lax.axis_size("ep")
    T, width = tokens.shape
    D4 = width // RING
    DC = D4 // C
    slots = n_ep * CAP
    R = slots * RING
    inner = w_down.shape[1]
    per = CAP * RING

    p1 = np.zeros((n_ep * 16, R), np.float32)
    p2 = np.zeros((R, n_ep * 16), np.float32)
    for e in range(n_ep):
        for s in range(RING):
            for q in range(CAP):
                p1[e * 16 + s * CAP + q, s * slots + e * CAP + q] = 1
        for j in range(per):
            p2[e * per + j, e * 16 + j] = 1
    consts = [jnp.asarray(m, BF16) for m in (p1, p1.T, p2, p2.T)]

    vm = pl.BlockSpec(memory_space=pltpu.VMEM)
    anyspec = pl.BlockSpec(memory_space=pl.ANY)
    V = pltpu.VMEM
    DMA = pltpu.SemaphoreType.DMA
    half = R // 2
    scratch = [
        V((T, width), BF16),
        V((C, 3, slots, DC), BF16),
        V((C, R, DC), BF16),
        V((C, n_ep * 16, DC), BF16),
        V((C, n_ep * 16, DC), BF16),
        V((C, RING * R, DC), BF16),
        V((RING, D4, 2 * inner), BF16),
        V((C, RING * inner, DC), BF16),
        V((RING, 3, R, 2 * inner), BF16),
        V((RING, R, 2 * inner), F32),
        V((RING, 3, R, 2 * inner), BF16),
        V((RING, R, RING * inner), BF16),
        V((C, R, DC), F32),
        V((C, R, DC), BF16),
        V((C, R, DC), BF16),
        V((C, R, DC), BF16),
        V((C, 2, half, DC), BF16),
        V((C, 2, half, DC), BF16),
        V((C, 2, half, DC), BF16),
        V((C, n_ep * 16, DC), BF16),
        V((C, n_ep * 16, DC), BF16),
        V((C, R, DC), BF16),
        DMA((3 + C,)), DMA((2 + C, 3)), DMA((2 + C, 3)), DMA((C, 3)), DMA((C, 3)),
        DMA((C, n_ep - 1)), DMA((C, n_ep - 1)), DMA((C, 6)), DMA((C, 6)),
        DMA((4, 3)), DMA((4, 3)), DMA((4, 3)), DMA((4, 3)), DMA((C, 6)), DMA((C, 6)),
        DMA((C, n_ep - 1)), DMA((C, n_ep - 1)), DMA((C, 3)), DMA((C, 3)),
    ]
    ret, scal = pl.pallas_call(
        kernel,
        out_shape=(jax.ShapeDtypeStruct((slots, width), BF16), jax.ShapeDtypeStruct((slots, T), F32)),
        in_specs=[vm] * 6 + [anyspec] * 4,
        out_specs=(vm, vm),
        scratch_shapes=scratch,
        compiler_params=pltpu.CompilerParams(collective_id=0, has_side_effects=True, vmem_limit_bytes=60 * 1024 * 1024),
        name="experts",
    )(expert_ids.T, gate_q.T, *consts, tokens, w_gate, w_up, w_down)
    mixed = lax.dot_general(scal, ret.astype(F32), (((0,), (0,)), ((), ())))
    return mixed.astype(BF16)


def solution(mesh):
    in_specs = (
        P(("ep", "etp"), None),
        P(("ep", "etp"), None),
        P(("ep", "etp"), None),
        P("ep", None, "etp"),
        P("ep", None, "etp"),
        P("ep", "etp", None),
    )
    out_specs = P(("ep", "etp"), None)
    return jax.shard_map(body, mesh=mesh, in_specs=in_specs, out_specs=out_specs, check_vma=False)
```

time: 181 us -> 154 us (0.85)
  Pallas kernels: 178 us -> 151 us
    pallas_call x1, Pallas kernels: 178 us -> 151 us  [body(): pl.pallas_call(kernel, out_shape=(jax.ShapeDtypeStruct((slots, width), BF...]
where the time goes in v2:
time: 154 us
  Pallas kernels  151 us (98%)
  matrix products  3.01 us (2%)
    pallas_call x1, Pallas kernels, body(): pl.pallas_call(kernel, out_shape=(jax.ShapeDtypeStruct((slots, width), BF...  151 us

profile of v2, /device:TPU:1, one launch (start us, length us, event | category | flops | bytes accessed | tf_op | source)
XLA Modules:
  0.0 154.2 jit_solution(6963212595743823008)
XLA Ops:
  0.0 151.2 %experts.1 = (bf16[48,7168]{1,0:T(8,128)(2,1)}, f32[48,128]{1,0:T(8,128)}) custom-call(s32[8,128]{1,0:T(8,128)} %bitcast.4, s32[8,128]{1,0:T(8,128)} %bitcast.5, bf16[256,192]{1,0:T(8,128)(2,1)} %constant.8.clone.p1_ref, bf16[192,256]{1,0:T(8,128)(2,1)} %constant.9.clone.p1t_ref, bf16[192,256]{1,0:T(8,128)(2,1)} %constant.10.clone.p2_ref, ...), custom_call_target="tpu_custom_call" | custom-call | tf_op jit(solution)/shard_map/experts/pallas_call | solution.py:388
  151.2 3.0 %fusion = bf16[128,7168]{1,0:T(8,128)(2,1)} fusion(f32[48,128]{1,0:T(8,128)} %get-tuple-element.7, bf16[48,7168]{1,0:T(8,128)(2,1)} %get-tuple-element.8), kind=kOutput, calls=%fused_computation.1 | convolution fusion | flops 88080384 | bytes 2547712 | tf_op jit(solution)/shard_map/dot_general | solution.py:397

commit v3 on v2

--- a/solution.py
+++ b/solution.py
@@ -9,6 +9,7 @@
 CAP = 3
 RING = 4
 C = 2
+CHUNKS = (4, 4, 3, 3)
 MESH = pl.DeviceIdType.MESH
 F32 = jnp.float32
 BF16 = jnp.bfloat16
@@ -25,7 +26,7 @@
 
 def kernel(ids_ref, gate_ref, p1_ref, p1t_ref, p2_ref, p2t_ref, tok_hbm, wg_hbm, wu_hbm, wd_hbm,
            ret_ref, scal_ref,
-           tok, bs, xa, sb, rb, X, wgu, wd, gp, own, hr, H, pown, pfar, pnear, pcomb, rfar, rdir, rcomb,
+           tok, bs, xa, sb, rb, X, wgu, wd, gp, own, hr, H, pfar, pnear, pcomb, rfar, rdir, rcomb,
            sr, rr, ts,
            loc_sem, w_send, w_recv, a_send, a_recv, b_send, b_recv, z_send, z_recv, g_send, g_recv,
            h_send, h_recv, r_send, r_recv, c_send, c_recv, d_send, d_recv):
@@ -40,7 +41,7 @@
     slots = n_ep * CAP
     R = slots * RING
     half = R // 2
-    inner = wd.shape[1] // RING
+    inner = wd.shape[0] // RING
 
     def xdev(k):
         return (ep, zi * RING + lax.rem(x + k, RING))
@@ -50,6 +51,13 @@
 
     def edev(k):
         return (lax.rem(ep + k, n_ep), etp)
+
+    part = D4 // sum(CHUNKS)
+    out = []
+    for n in CHUNKS:
+        out.append((sum(w for _, w in out), n * part))
+    Q = len(out)
+    others = (n_ep - 1) * 16
 
     everything = []
 
@@ -60,6 +68,13 @@
         everything.append(c)
         return c
 
+    def send_group(src, dst, ssem, rsem, dev):
+        pltpu.make_async_remote_copy(src_ref=src, dst_ref=dst, send_sem=ssem, recv_sem=rsem,
+                                     device_id=dev, device_id_type=MESH).start()
+
+    def wait_bytes(ref, sem):
+        pltpu.make_async_copy(ref, ref, sem).wait()
+
     def rows(start, size):
         return pl.ds(pl.multiple_of(start, 16), size)
 
@@ -72,8 +87,8 @@
         pltpu.make_async_copy(wg_hbm.at[0, rows(x * D4, D4), :], wgu.at[x, :, pl.ds(0, inner)], loc_sem.at[1]),
         pltpu.make_async_copy(wu_hbm.at[0, rows(x * D4, D4), :], wgu.at[x, :, pl.ds(inner, inner)], loc_sem.at[2]),
     ] + [
-        pltpu.make_async_copy(wd_hbm.at[0, :, cols(x * D4 + q * DC, DC)], wd.at[q, rows(x * inner, inner), :], loc_sem.at[3 + q])
-        for q in range(C)
+        pltpu.make_async_copy(wd_hbm.at[0, :, cols(x * D4 + o, w)], wd.at[rows(x * inner, inner), pl.ds(o, w)], loc_sem.at[3 + q])
+        for q, (o, w) in enumerate(out)
     ]
 
     barrier = pltpu.get_barrier_semaphore()
@@ -97,25 +112,28 @@
     before = lax.broadcasted_iota(jnp.int32, (T, T), 0) < lax.broadcasted_iota(jnp.int32, (T, T), 1)
     earlier = dot(hot.astype(BF16), jnp.where(before, 1.0, 0.0).astype(BF16))
     placing = jnp.where(earlier == slot, hot, 0.0)
-    scal_ref[...] = placing * weight * (1.0 / 1024.0)
+    scal_ref[...] = (placing * weight * (1.0 / 1024.0)).astype(BF16)
     placing = placing.astype(BF16)
 
     with scope("tokwait"):
         tok_copy.wait()
-    with scope("barrier_in"):
-        pl.semaphore_wait(barrier, (RING - 1) + 2 + (n_ep - 1))
-
-    a_copies = [[], []]
-    for q in range(C):
+    def bucket(q):
         for k in (2, 1, 3, 0):
-            dst_x = lax.rem(x + k, RING)
-            piece = dot(placing, tok[:, cols(dst_x * D4 + q * DC, DC)]).astype(BF16)
+            piece = dot(placing, tok[:, cols(lax.rem(x + k, RING) * D4 + q * DC, DC)]).astype(BF16)
             if k == 0:
                 xa[q, rows(x * slots, slots), :] = piece
             else:
                 bs[q, k - 1] = piece
-                a_copies[q].append(send(bs.at[q, k - 1], xa.at[q, rows(x * slots, slots), :],
-                                        a_send.at[q, k - 1], a_recv.at[q, k - 1], xdev(k)))
+
+    for q in range(C):
+        bucket(q)
+    with scope("barrier_in"):
+        pl.semaphore_wait(barrier, (RING - 1) + 2 + (n_ep - 1))
+    a_copies = [[], []]
+    for q in range(C):
+        for k in (2, 1, 3):
+            a_copies[q].append(send(bs.at[q, k - 1], xa.at[q, rows(x * slots, slots), :],
+                                    a_send.at[q, k - 1], a_recv.at[q, k - 1], xdev(k)))
 
     w_copies = []
     for i, k in enumerate((1, 3, 2)):
@@ -126,19 +144,19 @@
                              w_send.at[1, i], w_recv.at[1, i], xdev(k)))
 
     def send_down(q):
-        out = []
+        o, w = out[q]
+        copies = []
         for i, k in enumerate((1, 3, 2)):
             dst_x = lax.rem(x + k, RING)
-            out.append(send(wd_hbm.at[0, :, cols(dst_x * D4 + q * DC, DC)],
-                            wd.at[q, rows(x * inner, inner), :],
-                            w_send.at[2 + q, i], w_recv.at[2 + q, i], xdev(k)))
-        return out
+            copies.append(send(wd_hbm.at[0, :, cols(dst_x * D4 + o, w)],
+                               wd.at[rows(x * inner, inner), pl.ds(o, w)],
+                               w_send.at[2 + q, i], w_recv.at[2 + q, i], xdev(k)))
+        return copies
 
     d_copies = [send_down(0)]
     for cp in w_loc:
         cp.start()
 
-    b_copies = [[], []]
     for q in range(C):
         with scope("A_wait"):
             for cp in a_copies[q]:
@@ -146,8 +164,8 @@
         sb[q] = dot(p1_ref[...], xa[q]).astype(BF16)
         for k in range(1, n_ep):
             dst_e = lax.rem(ep + k, n_ep)
-            b_copies[q].append(send(sb.at[q, rows(dst_e * 16, 16), :], rb.at[q, rows(ep * 16, 16), :],
-                                    b_send.at[q, k - 1], b_recv.at[q, k - 1], edev(k)))
+            send_group(sb.at[q, rows(dst_e * 16, 16), :], rb.at[q, rows(ep * 16, 16), :],
+                       b_send.at[q], b_recv.at[q], edev(k))
         rb[q, rows(ep * 16, 16), :] = sb[q, rows(ep * 16, 16), :]
 
     zm = lax.rem(zi + RING - 1, RING)
@@ -165,8 +183,7 @@
     zc = [[None] * 6 for _ in range(C)]
     for q in range(C):
         with scope("B_wait"):
-            for cp in b_copies[q]:
-                cp.wait_recv()
+            wait_bytes(rb.at[q, pl.ds(0, others), :], b_recv.at[q])
         X[q, rows(zi * R, R), :] = dot(p2_ref[...], rb[q]).astype(BF16)
         zc[q][0] = zsend(q, zi, 0, 0, UP)
         zc[q][3] = zsend(q, zi, 1, 3, DOWN)
@@ -240,96 +257,115 @@
             w_loc[2 + q].wait()
 
     def down(i, q):
-        return dot(H[i], wd[q])
-
-    rc = [[None] * 6 for _ in range(C)]
+        o, w = out[q]
+        return dot(H[i], wd[:, pl.ds(o, w)])
+
+    rc = [[None] * 6 for _ in range(Q)]
 
     def rsend(buf, into, q, step):
+        o, w = out[q]
         for j, k in ((0, UP), (1, DOWN)):
             i = step + 3 * j
-            rc[q][i] = send(buf.at[q, pl.ds(j * half, half), :], into.at[q, j],
+            rc[q][i] = send(buf.at[pl.ds(j * half, half), pl.ds(o, w)], into.at[j, :, pl.ds(o, w)],
                             r_send.at[q, i], r_recv.at[q, i], zdev(k))
 
     def near(q):
+        o, w = out[q]
         with scope("near%d" % q):
-            pnear[q] = down(N, q).astype(BF16)
+            pnear[:, pl.ds(o, w)] = down(N, q).astype(BF16)
+            rsend(pnear, rdir, q, 1)
 
     def far(q):
+        o, w = out[q]
         with scope("far%d" % q):
-            pfar[q] = down(F, q).astype(BF16)
+            pfar[:, pl.ds(o, w)] = down(F, q).astype(BF16)
             rsend(pfar, rfar, q, 0)
 
     def combine(q):
+        o, w = out[q]
+        sl = pl.ds(o, w)
         with scope("comb%d" % q):
             part = down(M, q)
         with scope("S1w%d" % q):
             rc[q][0].wait_recv()
             rc[q][3].wait_recv()
         for j in range(2):
-            pcomb[q, pl.ds(j * half, half), :] = (part[j * half:(j + 1) * half] + rfar[q, j].astype(F32)).astype(BF16)
+            pcomb[pl.ds(j * half, half), sl] = (part[j * half:(j + 1) * half] + rfar[j, :, sl].astype(F32)).astype(BF16)
         rsend(pcomb, rcomb, q, 2)
 
+    def finish(q):
+        o, w = out[q]
+        sl = pl.ds(o, w)
+        mine = down(O, q)
+        with scope("S3w%d" % q):
+            for i in (1, 4, 2, 5):
+                rc[q][i].wait_recv()
+        y_lo = mine[:half] + rcomb[0, :, sl].astype(F32) + rdir[1, :, sl].astype(F32)
+        y_hi = mine[half:] + rcomb[1, :, sl].astype(F32) + rdir[0, :, sl].astype(F32)
+        y = jnp.concatenate([y_lo.astype(BF16), y_hi.astype(BF16)], axis=0)
+        sr[:, sl] = dot(p2t_ref[...], y).astype(BF16)
+        for k in range(1, n_ep):
+            dst_e = lax.rem(ep + k, n_ep)
+            send_group(sr.at[rows(dst_e * 16, 16), sl], rr.at[rows(ep * 16, 16), sl],
+                       c_send.at[q], c_recv.at[q], edev(k))
+        rr[rows(ep * 16, 16), sl] = sr[rows(ep * 16, 16), sl]
+
+    dc = []
+
+    def give_back(q):
+        o, w = out[q]
+        sl = pl.ds(o, w)
+        with scope("RBw%d" % q):
+            wait_bytes(rr.at[pl.ds(0, others), sl], c_recv.at[q])
+        ts[:, sl] = dot(p1t_ref[...], rr[:, sl]).astype(BF16)
+        for k in (2, 1, 3):
+            dst_x = lax.rem(x + k, RING)
+            dc.append(send(ts.at[rows(dst_x * slots, slots), sl], ret_ref.at[:, cols(x * D4 + o, w)],
+                           d_send.at[q, k - 1], d_recv.at[q, k - 1], xdev(k)))
+        ret_ref[:, cols(x * D4 + o, w)] = ts[rows(x * slots, slots), sl]
+
     first(N)
-    first(O)
-    second(N)
     zwait(2, 5)
     first(F)
-    zwait(1, 4)
-    first(M)
+    second(N)
+    second(F)
+    for q in range(1, Q):
+        d_copies.append(send_down(q))
     hwait(N)
     dwait(0)
     near(0)
-    rsend(pnear, rdir, 0, 1)
-    second(F)
-    d_copies.append(send_down(1))
+    hwait(F)
+    far(0)
+    zwait(1, 4)
+    first(M)
+    first(O)
+    for q in range(1, Q):
+        dwait(q)
+        near(q)
+        far(q)
     second(M)
     second(O)
-    hwait(F)
-    far(0)
-    dwait(1)
-    far(1)
-    near(1)
     hwait(M)
-    combine(0)
-    rsend(pnear, rdir, 1, 1)
-    combine(1)
+    for q in range(Q):
+        combine(q)
     hwait(O)
-    with scope("own"):
-        for q in range(C):
-            pown[q] = down(O, q)
-
-    cc = [[], []]
-    for q in range(C):
-        with scope("S3w"):
-            for i in (1, 4, 2, 5):
-                rc[q][i].wait_recv()
-        y_lo = pown[q, pl.ds(0, half), :] + rcomb[q, 0].astype(F32) + rdir[q, 1].astype(F32)
-        y_hi = pown[q, pl.ds(half, half), :] + rcomb[q, 1].astype(F32) + rdir[q, 0].astype(F32)
-        y = jnp.concatenate([y_lo.astype(BF16), y_hi.astype(BF16)], axis=0)
-        sr[q] = dot(p2t_ref[...], y).astype(BF16)
-        for k in range(1, n_ep):
-            dst_e = lax.rem(ep + k, n_ep)
-            cc[q].append(send(sr.at[q, rows(dst_e * 16, 16), :], rr.at[q, rows(ep * 16, 16), :],
-                              c_send.at[q, k - 1], c_recv.at[q, k - 1], edev(k)))
-        rr[q, rows(ep * 16, 16), :] = sr[q, rows(ep * 16, 16), :]
-    dc = [[], []]
-    for q in range(C):
-        with scope("RBw"):
-            for cp in cc[q]:
-                cp.wait_recv()
-        ts[q] = dot(p1t_ref[...], rr[q]).astype(BF16)
-        for k in (2, 1, 3):
-            dst_x = lax.rem(x + k, RING)
-            dc[q].append(send(ts.at[q, rows(dst_x * slots, slots), :], ret_ref.at[:, cols(x * D4 + q * DC, DC)],
-                              d_send.at[q, k - 1], d_recv.at[q, k - 1], xdev(k)))
-        ret_ref[:, cols(x * D4 + q * DC, DC)] = ts[q, rows(x * slots, slots), :]
+    finish(0)
+    finish(1)
+    for q in range(2, Q):
+        give_back(q - 2)
+        finish(q)
+    give_back(Q - 2)
+    give_back(Q - 1)
     with scope("RAw"):
-        for q in range(C):
-            for cp in dc[q]:
-                cp.wait_recv()
+        for cp in dc:
+            cp.wait_recv()
     with scope("sends"):
         for cp in everything:
             cp.wait_send()
+        for q in range(C):
+            wait_bytes(sb.at[q, pl.ds(0, others), :], b_send.at[q])
+        for q, (o, w) in enumerate(out):
+            wait_bytes(sr.at[pl.ds(0, others), pl.ds(o, w)], c_send.at[q])
 
 
 def body(tokens, expert_ids, gate_q, w_gate, w_up, w_down):
@@ -357,6 +393,7 @@
     V = pltpu.VMEM
     DMA = pltpu.SemaphoreType.DMA
     half = R // 2
+    Q = len(CHUNKS)
     scratch = [
         V((T, width), BF16),
         V((C, 3, slots, DC), BF16),
@@ -365,36 +402,35 @@
         V((C, n_ep * 16, DC), BF16),
         V((C, RING * R, DC), BF16),
         V((RING, D4, 2 * inner), BF16),
-        V((C, RING * inner, DC), BF16),
+        V((RING * inner, D4), BF16),
         V((RING, 3, R, 2 * inner), BF16),
         V((RING, R, 2 * inner), F32),
         V((RING, 3, R, 2 * inner), BF16),
         V((RING, R, RING * inner), BF16),
-        V((C, R, DC), F32),
-        V((C, R, DC), BF16),
-        V((C, R, DC), BF16),
-        V((C, R, DC), BF16),
-        V((C, 2, half, DC), BF16),
-        V((C, 2, half, DC), BF16),
-        V((C, 2, half, DC), BF16),
-        V((C, n_ep * 16, DC), BF16),
-        V((C, n_ep * 16, DC), BF16),
-        V((C, R, DC), BF16),
-        DMA((3 + C,)), DMA((2 + C, 3)), DMA((2 + C, 3)), DMA((C, 3)), DMA((C, 3)),
-        DMA((C, n_ep - 1)), DMA((C, n_ep - 1)), DMA((C, 6)), DMA((C, 6)),
-        DMA((4, 3)), DMA((4, 3)), DMA((4, 3)), DMA((4, 3)), DMA((C, 6)), DMA((C, 6)),
-        DMA((C, n_ep - 1)), DMA((C, n_ep - 1)), DMA((C, 3)), DMA((C, 3)),
+        V((R, D4), BF16),
+        V((R, D4), BF16),
+        V((R, D4), BF16),
+        V((2, half, D4), BF16),
+        V((2, half, D4), BF16),
+        V((2, half, D4), BF16),
+        V((n_ep * 16, D4), BF16),
+        V((n_ep * 16, D4), BF16),
+        V((R, D4), BF16),
+        DMA((3 + Q,)), DMA((2 + Q, 3)), DMA((2 + Q, 3)), DMA((C, 3)), DMA((C, 3)),
+        DMA((C,)), DMA((C,)), DMA((C, 6)), DMA((C, 6)),
+        DMA((4, 3)), DMA((4, 3)), DMA((4, 3)), DMA((4, 3)), DMA((Q, 6)), DMA((Q, 6)),
+        DMA((Q,)), DMA((Q,)), DMA((Q, 3)), DMA((Q, 3)),
     ]
     ret, scal = pl.pallas_call(
         kernel,
-        out_shape=(jax.ShapeDtypeStruct((slots, width), BF16), jax.ShapeDtypeStruct((slots, T), F32)),
+        out_shape=(jax.ShapeDtypeStruct((slots, width), BF16), jax.ShapeDtypeStruct((slots, T), BF16)),
         in_specs=[vm] * 6 + [anyspec] * 4,
         out_specs=(vm, vm),
         scratch_shapes=scratch,
         compiler_params=pltpu.CompilerParams(collective_id=0, has_side_effects=True, vmem_limit_bytes=60 * 1024 * 1024),
         name="experts",
     )(expert_ids.T, gate_q.T, *consts, tokens, w_gate, w_up, w_down)
-    mixed = lax.dot_general(scal, ret.astype(F32), (((0,), (0,)), ((), ())))
+    mixed = lax.dot_general(scal, ret, (((0,), (0,)), ((), ())), preferred_element_type=F32)
     return mixed.astype(BF16)
 
 

time: 154 us -> 146 us (0.948)
  Pallas kernels: 151 us -> 143 us
    pallas_call x1, Pallas kernels: 151 us -> 143 us  [body(): pl.pallas_call(kernel, out_shape=(jax.ShapeDtypeStruct((slots, width), BF...]
where the time goes in v3:
time: 146 us
  Pallas kernels  143 us (98%)
  matrix products  3.01 us (2%)
    pallas_call x1, Pallas kernels, body(): pl.pallas_call(kernel, out_shape=(jax.ShapeDtypeStruct((slots, width), BF...  143 us
    dot_general x1, matrix products, body(): lax.dot_general(scal, ret, (((0,), (0,)), ((), ())), preferred_element_ty...  3.01 us

profile of v3, /device:TPU:1, one launch (start us, length us, event | category | flops | bytes accessed | tf_op | source)
XLA Modules:
  0.0 145.8 jit_solution(3933454639295373614)
XLA Ops:
  0.0 142.8 %experts.1 = (bf16[48,7168]{1,0:T(8,128)(2,1)}, bf16[48,128]{1,0:T(8,128)(2,1)}) custom-call(s32[8,128]{1,0:T(8,128)} %bitcast.4, s32[8,128]{1,0:T(8,128)} %bitcast.5, bf16[256,192]{1,0:T(8,128)(2,1)} %constant.8.clone.p1_ref, bf16[192,256]{1,0:T(8,128)(2,1)} %constant.9.clone.p1t_ref, bf16[192,256]{1,0:T(8,128)(2,1)} %constant.10.clone.p2_ref, ...), custom_call_target="tpu_custom_call" | custom-call | tf_op jit(solution)/shard_map/experts/pallas_call | solution.py:424
  142.8 3.0 %convolution_convert_fusion = bf16[128,7168]{1,0:T(8,128)(2,1)} fusion(bf16[48,128]{1,0:T(8,128)(2,1)} %get-tuple-element.7, bf16[48,7168]{1,0:T(8,128)(2,1)} %get-tuple-element.8), kind=kOutput, calls=%fused_computation | convolution fusion | flops 88997888 | bytes 2535424 | tf_op jit(solution)/shard_map/dot_general | solution.py:433

commit v4 on v3

v4 whole, which is shorter than its diff:
```python
import jax
import jax.numpy as jnp
import numpy as np
from jax import lax
from jax.experimental import pallas as pl
from jax.experimental.pallas import tpu as pltpu
from jax.sharding import PartitionSpec as P

CAP = 3
RING = 4
CIN = (3, 4, 4, 3)
CHUNKS = (3, 4, 4, 3)
MESH = pl.DeviceIdType.MESH
F32 = jnp.float32
BF16 = jnp.bfloat16
scope = jax.named_scope


def third(c):
    return lax.shift_right_logical(c * 43691, 17)


def dot(a, b):
    return jnp.dot(a, b, preferred_element_type=F32)


def kernel(ids_ref, gate_ref, p1_ref, p1t_ref, p2_ref, p2t_ref, tok_hbm, wg_hbm, wu_hbm, wd_hbm,
           ret_ref, scal_ref,
           tok, bs, xa, sb, rb, X, wgu, wd, gp, own, hr, H, pfar, pnear, pcomb, rfar, rdir, rcomb,
           sr, rr, ts,
           loc_sem, send_sem, w_recv, wd_recv, a_recv, b_recv, zn_recv, zf_recv, zm_recv, g_recv,
           h_recv, rf_recv, ro_recv, c_recv, d_recv):
    ep = lax.axis_index("ep")
    etp = lax.axis_index("etp")
    n_ep = lax.axis_size("ep")
    zi = etp // RING
    x = etp % RING
    width = tok.shape[1]
    D4 = width // RING
    slots = n_ep * CAP
    R = slots * RING
    half = R // 2
    inner = wd.shape[0] // RING

    def xdev(k):
        return (ep, zi * RING + lax.rem(x + k, RING))

    def zdev(k):
        return (ep, lax.rem(zi + k, RING) * RING + x)

    def edev(k):
        return (lax.rem(ep + k, n_ep), etp)

    def spans(parts):
        made = []
        for n in parts:
            made.append((sum(w for _, w in made), n * D4 // sum(parts)))
        return made

    into, out = spans(CIN), spans(CHUNKS)
    C, Q = len(into), len(out)
    others = (n_ep - 1) * 16

    A_S, W_S, D_S, B_S, Z_S, G_S, H_S, R_S, C_S, E_S = range(10)

    def send(src, dst, group, rsem, dev):
        pltpu.make_async_remote_copy(src_ref=src, dst_ref=dst, send_sem=send_sem.at[group], recv_sem=rsem,
                                     device_id=dev, device_id_type=MESH).start()

    def wait_bytes(ref, sem):
        pltpu.make_async_copy(ref, ref, sem).wait()

    def rows(start, size):
        return pl.ds(pl.multiple_of(start, 16), size)

    def cols(start, size):
        return pl.ds(pl.multiple_of(start, 128), size)

    tok_copy = pltpu.make_async_copy(tok_hbm, tok, loc_sem.at[0])
    tok_copy.start()
    w_loc = [
        pltpu.make_async_copy(wg_hbm.at[0, rows(x * D4, D4), :], wgu.at[x, :, pl.ds(0, inner)], loc_sem.at[1]),
        pltpu.make_async_copy(wu_hbm.at[0, rows(x * D4, D4), :], wgu.at[x, :, pl.ds(inner, inner)], loc_sem.at[2]),
    ] + [
        pltpu.make_async_copy(wd_hbm.at[0, :, cols(x * D4 + o, w)], wd.at[rows(x * inner, inner), pl.ds(o, w)], loc_sem.at[3 + q])
        for q, (o, w) in enumerate(out)
    ]

    barrier = pltpu.get_barrier_semaphore()
    for k in range(1, RING):
        pl.semaphore_signal(barrier, inc=1, device_id=xdev(k), device_id_type=MESH)
    for k in (1, RING - 1):
        pl.semaphore_signal(barrier, inc=1, device_id=zdev(k), device_id_type=MESH)
    for k in range(1, n_ep):
        pl.semaphore_signal(barrier, inc=1, device_id=edev(k), device_id_type=MESH)

    T = tok.shape[0]
    c = lax.broadcasted_iota(jnp.int32, (slots, T), 0)
    expert = third(c)
    slot = (c - CAP * expert).astype(F32)
    hot = jnp.zeros((slots, T), F32)
    weight = jnp.zeros((slots, T), F32)
    for r in range(ids_ref.shape[0]):
        eq = ids_ref[r:r + 1, :] == expert
        hot = jnp.where(eq, 1.0, hot)
        weight = jnp.where(eq, gate_ref[r:r + 1, :].astype(F32), weight)
    before = lax.broadcasted_iota(jnp.int32, (T, T), 0) < lax.broadcasted_iota(jnp.int32, (T, T), 1)
    earlier = dot(hot.astype(BF16), jnp.where(before, 1.0, 0.0).astype(BF16))
    placing = jnp.where(earlier == slot, hot, 0.0)
    scal_ref[...] = (placing * weight * (1.0 / 1024.0)).astype(BF16)
    placing = placing.astype(BF16)

    with scope("tokwait"):
        tok_copy.wait()
    def bucket(q):
        o, w = into[q]
        for k in (2, 1, 3, 0):
            piece = dot(placing, tok[:, cols(lax.rem(x + k, RING) * D4 + o, w)]).astype(BF16)
            if k == 0:
                xa[rows(x * slots, slots), pl.ds(o, w)] = piece
            else:
                bs[k - 1, :, pl.ds(o, w)] = piece

    for q in range(C):
        bucket(q)
    with scope("barrier_in"):
        pl.semaphore_wait(barrier, (RING - 1) + 2 + (n_ep - 1))
    for q, (o, w) in enumerate(into):
        for k in (2, 1, 3):
            send(bs.at[k - 1, :, pl.ds(o, w)], xa.at[rows(x * slots, slots), pl.ds(o, w)],
                 A_S, a_recv.at[q], xdev(k))

    for k in (1, 3, 2):
        dst_x = lax.rem(x + k, RING)
        send(wg_hbm.at[0, rows(dst_x * D4, D4), :], wgu.at[x, :, pl.ds(0, inner)], W_S, w_recv, xdev(k))
        send(wu_hbm.at[0, rows(dst_x * D4, D4), :], wgu.at[x, :, pl.ds(inner, inner)], W_S, w_recv, xdev(k))

    def send_down(q):
        o, w = out[q]
        for k in (1, 3, 2):
            dst_x = lax.rem(x + k, RING)
            send(wd_hbm.at[0, :, cols(dst_x * D4 + o, w)], wd.at[rows(x * inner, inner), pl.ds(o, w)],
                 D_S, wd_recv.at[q], xdev(k))

    send_down(0)
    for cp in w_loc:
        cp.start()

    for q, (o, w) in enumerate(into):
        sl = pl.ds(o, w)
        with scope("A_wait"):
            wait_bytes(xa.at[pl.ds(0, (RING - 1) * slots), sl], a_recv.at[q])
        sb[:, sl] = dot(p1_ref[...], xa[:, sl]).astype(BF16)
        for k in range(1, n_ep):
            dst_e = lax.rem(ep + k, n_ep)
            send(sb.at[rows(dst_e * 16, 16), sl], rb.at[rows(ep * 16, 16), sl], B_S, b_recv.at[q], edev(k))
        rb[rows(ep * 16, 16), sl] = sb[rows(ep * 16, 16), sl]

    zm = lax.rem(zi + RING - 1, RING)
    zp = lax.rem(zi + 1, RING)
    zf = lax.rem(zi + 2, RING)

    def unit(b, h):
        return rows((2 * b + h) * half, half)

    def zsend(q, b, h, rsem, k):
        part = X.at[unit(b, h), pl.ds(*into[q])]
        send(part, part, Z_S, rsem, zdev(k))

    def zwait(sem, q, count):
        wait_bytes(X.at[pl.ds(0, count * half), pl.ds(*into[q])], sem)

    UP, DOWN = 1, RING - 1

    def outset(q):
        sl = pl.ds(*into[q])
        with scope("B_wait"):
            wait_bytes(rb.at[pl.ds(0, others), sl], b_recv.at[q])
        X[rows(zi * R, R), sl] = dot(p2_ref[...], rb[:, sl]).astype(BF16)
        zsend(q, zi, 0, zn_recv.at[q, 0], UP)
        zsend(q, zi, 1, zn_recv.at[q, 1], DOWN)

    def forward(q):
        with scope("Z0_wait"):
            zwait(zn_recv.at[q, 0], q, 1)
        zsend(q, zm, 0, zf_recv.at[q], UP)
        with scope("Z3_wait"):
            zwait(zn_recv.at[q, 1], q, 1)
        zsend(q, zp, 1, zf_recv.at[q], DOWN)

    for q in range(C):
        outset(q)
    for q in range(C):
        forward(q)
    for q in range(C):
        zsend(q, zi, 1, zm_recv.at[q], UP)
        zsend(q, zi, 0, zm_recv.at[q], DOWN)

    with scope("W_wait"):
        wait_bytes(wgu.at[pl.ds(0, RING - 1)], w_recv)
        w_loc[0].wait()
        w_loc[1].wait()

    N, F, M, O = range(4)
    pairs = [((zp, 1), (zm, 0)), ((zf, 0), (zf, 1)), ((zp, 0), (zm, 1)), ((zi, 0), (zi, 1))]
    def first(i):
        with scope("first%d" % i):
            xs = jnp.concatenate([X[unit(*u), :] for u in pairs[i]], axis=0)
            for k in (2, 1, 3, 0):
                dst_x = lax.rem(x + k, RING)
                acc = dot(xs, wgu[dst_x])
                if k == 0:
                    own[i] = acc
                else:
                    gp[i, k - 1] = acc.astype(BF16)
                    send(gp.at[i, k - 1], hr.at[i, k - 1], G_S, g_recv.at[i], xdev(k))

    def second(i):
        with scope("gwait%d" % i):
            wait_bytes(hr.at[i], g_recv.at[i])
        with scope("second%d" % i):
            total = own[i]
            for k in range(RING - 1):
                total = total + hr[i, k].astype(F32)
            g = total[:, :inner]
            u = total[:, inner:]
            part = H.at[i, :, cols(x * inner, inner)]
            part[...] = (g / (1.0 + jnp.exp(-g)) * u).astype(BF16)
            for k in (2, 1, 3):
                send(part, part, H_S, h_recv.at[i], xdev(k))

    def hwait(i):
        with scope("hwait%d" % i):
            wait_bytes(H.at[i, :, pl.ds(0, (RING - 1) * inner)], h_recv.at[i])

    def dwait(q):
        with scope("dwait%d" % q):
            wait_bytes(wd.at[pl.ds(0, (RING - 1) * inner), pl.ds(*out[q])], wd_recv.at[q])
            w_loc[2 + q].wait()

    def down(i, q):
        o, w = out[q]
        return dot(H[i], wd[:, pl.ds(o, w)])

    def rsend(buf, into, q, rsem):
        o, w = out[q]
        for j, k in ((0, UP), (1, DOWN)):
            send(buf.at[pl.ds(j * half, half), pl.ds(o, w)], into.at[j, :, pl.ds(o, w)], R_S, rsem, zdev(k))

    def near(q):
        o, w = out[q]
        with scope("near%d" % q):
            pnear[:, pl.ds(o, w)] = down(N, q).astype(BF16)
            rsend(pnear, rdir, q, ro_recv.at[q])

    def far(q):
        o, w = out[q]
        with scope("far%d" % q):
            pfar[:, pl.ds(o, w)] = down(F, q).astype(BF16)
            rsend(pfar, rfar, q, rf_recv.at[q])

    def combine(q):
        o, w = out[q]
        sl = pl.ds(o, w)
        with scope("comb%d" % q):
            part = down(M, q)
        with scope("S1w%d" % q):
            wait_bytes(X.at[pl.ds(0, 2 * half), sl], rf_recv.at[q])
        for j in range(2):
            pcomb[pl.ds(j * half, half), sl] = (part[j * half:(j + 1) * half] + rfar[j, :, sl].astype(F32)).astype(BF16)
        rsend(pcomb, rcomb, q, ro_recv.at[q])

    def finish(q):
        o, w = out[q]
        sl = pl.ds(o, w)
        mine = down(O, q)
        with scope("S3w%d" % q):
            wait_bytes(X.at[pl.ds(0, 4 * half), sl], ro_recv.at[q])
        y_lo = mine[:half] + rcomb[0, :, sl].astype(F32) + rdir[1, :, sl].astype(F32)
        y_hi = mine[half:] + rcomb[1, :, sl].astype(F32) + rdir[0, :, sl].astype(F32)
        y = jnp.concatenate([y_lo.astype(BF16), y_hi.astype(BF16)], axis=0)
        sr[:, sl] = dot(p2t_ref[...], y).astype(BF16)
        for k in range(1, n_ep):
            dst_e = lax.rem(ep + k, n_ep)
            send(sr.at[rows(dst_e * 16, 16), sl], rr.at[rows(ep * 16, 16), sl], C_S, c_recv.at[q], edev(k))
        rr[rows(ep * 16, 16), sl] = sr[rows(ep * 16, 16), sl]

    def give_back(q):
        o, w = out[q]
        sl = pl.ds(o, w)
        with scope("RBw%d" % q):
            wait_bytes(rr.at[pl.ds(0, others), sl], c_recv.at[q])
        ts[:, sl] = dot(p1t_ref[...], rr[:, sl]).astype(BF16)
        for k in (2, 1, 3):
            dst_x = lax.rem(x + k, RING)
            send(ts.at[rows(dst_x * slots, slots), sl], ret_ref.at[:, cols(x * D4 + o, w)], E_S, d_recv, xdev(k))
        ret_ref[:, cols(x * D4 + o, w)] = ts[rows(x * slots, slots), sl]

    first(N)
    with scope("zfwait"):
        for q in range(C):
            zwait(zf_recv.at[q], q, 2)
    first(F)
    second(N)
    second(F)
    send_down(1)
    send_down(2)
    hwait(N)
    dwait(0)
    near(0)
    hwait(F)
    far(0)
    with scope("zmwait"):
        for q in range(C):
            zwait(zm_recv.at[q], q, 2)
    first(M)
    send_down(3)
    for q in (1, 2):
        dwait(q)
        near(q)
        far(q)
    second(M)
    first(O)
    dwait(3)
    near(3)
    far(3)
    second(O)
    hwait(M)
    for q in range(Q):
        combine(q)
    hwait(O)
    finish(0)
    finish(1)
    for q in range(2, Q):
        give_back(q - 2)
        finish(q)
    give_back(Q - 2)
    give_back(Q - 1)
    with scope("RAw"):
        wait_bytes(ts.at[pl.ds(0, (RING - 1) * slots), :], d_recv)
    with scope("sends"):
        for group, ref in ((A_S, bs), (W_S, wgu.at[pl.ds(0, RING - 1)]),
                           (D_S, wd.at[pl.ds(0, (RING - 1) * inner), :]),
                           (B_S, sb.at[pl.ds(0, others), :]), (Z_S, X.at[pl.ds(0, 6 * half), :]),
                           (G_S, hr), (H_S, H.at[:, :, pl.ds(0, (RING - 1) * inner)]),
                           (R_S, X.at[pl.ds(0, 6 * half), :]), (C_S, sr.at[pl.ds(0, others), :]),
                           (E_S, ts.at[pl.ds(0, (RING - 1) * slots), :])):
            wait_bytes(ref, send_sem.at[group])


def body(tokens, expert_ids, gate_q, w_gate, w_up, w_down):
    n_ep = lax.axis_size("ep")
    T, width = tokens.shape
    D4 = width // RING
    slots = n_ep * CAP
    R = slots * RING
    inner = w_down.shape[1]
    per = CAP * RING

    p1 = np.zeros((n_ep * 16, R), np.float32)
    p2 = np.zeros((R, n_ep * 16), np.float32)
    for e in range(n_ep):
        for s in range(RING):
            for q in range(CAP):
                p1[e * 16 + s * CAP + q, s * slots + e * CAP + q] = 1
        for j in range(per):
            p2[e * per + j, e * 16 + j] = 1
    consts = [jnp.asarray(m, BF16) for m in (p1, p1.T, p2, p2.T)]

    vm = pl.BlockSpec(memory_space=pltpu.VMEM)
    anyspec = pl.BlockSpec(memory_space=pl.ANY)
    V = pltpu.VMEM
    DMA = pltpu.SemaphoreType.DMA
    half = R // 2
    C, Q = len(CIN), len(CHUNKS)
    scratch = [
        V((T, width), BF16),
        V((3, slots, D4), BF16),
        V((R, D4), BF16),
        V((n_ep * 16, D4), BF16),
        V((n_ep * 16, D4), BF16),
        V((RING * R, D4), BF16),
        V((RING, D4, 2 * inner), BF16),
        V((RING * inner, D4), BF16),
        V((RING, 3, R, 2 * inner), BF16),
        V((RING, R, 2 * inner), F32),
        V((RING, 3, R, 2 * inner), BF16),
        V((RING, R, RING * inner), BF16),
        V((R, D4), BF16),
        V((R, D4), BF16),
        V((R, D4), BF16),
        V((2, half, D4), BF16),
        V((2, half, D4), BF16),
        V((2, half, D4), BF16),
        V((n_ep * 16, D4), BF16),
        V((n_ep * 16, D4), BF16),
        V((R, D4), BF16),
        DMA((3 + Q,)), DMA((10,)), DMA(()), DMA((Q,)), DMA((C,)), DMA((C,)), DMA((C, 2)), DMA((C,)), DMA((C,)),
        DMA((4,)), DMA((4,)), DMA((Q,)), DMA((Q,)), DMA((Q,)), DMA(()),
    ]
    ret, scal = pl.pallas_call(
        kernel,
        out_shape=(pltpu.VMEM((slots, width), BF16), pltpu.VMEM((slots, T), BF16)),
        in_specs=[vm] * 6 + [anyspec] * 4,
        out_specs=(vm, vm),
        scratch_shapes=scratch,
        compiler_params=pltpu.CompilerParams(collective_id=0, has_side_effects=True, vmem_limit_bytes=60 * 1024 * 1024),
        name="experts",
    )(expert_ids.T, gate_q.T, *consts, tokens, w_gate, w_up, w_down)
    mixed = lax.dot_general(scal, ret, (((0,), (0,)), ((), ())), preferred_element_type=F32)
    return mixed.astype(BF16)


def solution(mesh):
    in_specs = (
        P(("ep", "etp"), None),
        P(("ep", "etp"), None),
        P(("ep", "etp"), None),
        P("ep", None, "etp"),
        P("ep", None, "etp"),
        P("ep", "etp", None),
    )
    out_specs = P(("ep", "etp"), None)
    return jax.shard_map(body, mesh=mesh, in_specs=in_specs, out_specs=out_specs, check_vma=False)
```

time: 146 us -> 141 us (0.966)
  Pallas kernels: 143 us -> 139 us
    pallas_call x1, Pallas kernels: 143 us -> 139 us  [body(): pl.pallas_call(kernel, out_shape=(pltpu.VMEM((slots, width), BF16), pltpu...]
where the time goes in v4:
time: 141 us
  Pallas kernels  139 us (99%)
  matrix products  1.89 us (1%)
    pallas_call x1, Pallas kernels, body(): pl.pallas_call(kernel, out_shape=(pltpu.VMEM((slots, width), BF16), pltpu...  139 us

profile of v4, /device:TPU:1, one launch (start us, length us, event | category | flops | bytes accessed | tf_op | source)
XLA Modules:
  0.0 141.1 jit_solution(12753269842494457863)
XLA Ops:
  0.0 139.2 %experts.1 = (bf16[48,7168]{1,0:T(8,128)(2,1)S(1)}, bf16[48,128]{1,0:T(8,128)(2,1)S(1)}) custom-call(s32[8,128]{1,0:T(8,128)} %bitcast.4, s32[8,128]{1,0:T(8,128)} %bitcast.5, bf16[256,192]{1,0:T(8,128)(2,1)} %constant.8.clone.p1_ref, bf16[192,256]{1,0:T(8,128)(2,1)} %constant.9.clone.p1t_ref, bf16[192,256]{1,0:T(8,128)(2,1)} %constant.10.clone.p2_ref, ...), custom_call_target="tpu_custom_call" | custom-call | tf_op jit(solution)/shard_map/experts/pallas_call | solution.py:401
  139.2 1.9 %convolution_convert_fusion = bf16[128,7168]{1,0:T(8,128)(2,1)} fusion(bf16[48,128]{1,0:T(8,128)(2,1)S(1)} %get-tuple-element.7, bf16[48,7168]{1,0:T(8,128)(2,1)S(1)} %get-tuple-element.8), kind=kOutput, calls=%fused_computation | convolution fusion | flops 88997888 | bytes 2535424 | tf_op jit(solution)/shard_map/dot_general | solution.py:410

commit v5 on v4

--- a/solution.py
+++ b/solution.py
@@ -8,8 +8,8 @@
 
 CAP = 3
 RING = 4
-CIN = (3, 4, 4, 3)
-CHUNKS = (3, 4, 4, 3)
+CIN = (4, 4, 4, 2)
+CHUNKS = (4, 4, 4, 2)
 MESH = pl.DeviceIdType.MESH
 F32 = jnp.float32
 BF16 = jnp.bfloat16
@@ -24,9 +24,32 @@
     return jnp.dot(a, b, preferred_element_type=F32)
 
 
-def kernel(ids_ref, gate_ref, p1_ref, p1t_ref, p2_ref, p2t_ref, tok_hbm, wg_hbm, wu_hbm, wd_hbm,
+def packed(width):
+    return width * 3 // 4 if width % 512 == 0 else width
+
+
+def pack(p, src):
+    w = src.shape[1]
+    keep = packed(w)
+    made = dot(p[0], src[:, :keep])
+    if keep < w:
+        made = made + jnp.concatenate([dot(p[1 + j], src[:, keep:]) for j in range(3)], axis=1)
+    return made.astype(BF16)
+
+
+def unpack(p, src, w):
+    keep = packed(w)
+    made = dot(p[0], src).astype(BF16)
+    if keep < w:
+        part = w - keep
+        rest = dot(p[1], src[:, :part]) + dot(p[2], src[:, part:2 * part]) + dot(p[3], src[:, 2 * part:])
+        made = jnp.concatenate([made, rest.astype(BF16)], axis=1)
+    return made
+
+
+def kernel(ids_hbm, gate_hbm, p1_hbm, p1t_hbm, p2_hbm, p2t_hbm, tok_hbm, wg_hbm, wu_hbm, wd_hbm,
            ret_ref, scal_ref,
-           tok, bs, xa, sb, rb, X, wgu, wd, gp, own, hr, H, pfar, pnear, pcomb, rfar, rdir, rcomb,
+           ids_ref, gate_ref, p1_ref, p1t_ref, p2_ref, p2t_ref, tok, bs, xa, sb, rb, X, wgu, wd, gp, own, hr, H, pfar, pnear, pcomb, rfar, rdir, rcomb,
            sr, rr, ts,
            loc_sem, send_sem, w_recv, wd_recv, a_recv, b_recv, zn_recv, zf_recv, zm_recv, g_recv,
            h_recv, rf_recv, ro_recv, c_recv, d_recv):
@@ -76,16 +99,6 @@
     def cols(start, size):
         return pl.ds(pl.multiple_of(start, 128), size)
 
-    tok_copy = pltpu.make_async_copy(tok_hbm, tok, loc_sem.at[0])
-    tok_copy.start()
-    w_loc = [
-        pltpu.make_async_copy(wg_hbm.at[0, rows(x * D4, D4), :], wgu.at[x, :, pl.ds(0, inner)], loc_sem.at[1]),
-        pltpu.make_async_copy(wu_hbm.at[0, rows(x * D4, D4), :], wgu.at[x, :, pl.ds(inner, inner)], loc_sem.at[2]),
-    ] + [
-        pltpu.make_async_copy(wd_hbm.at[0, :, cols(x * D4 + o, w)], wd.at[rows(x * inner, inner), pl.ds(o, w)], loc_sem.at[3 + q])
-        for q, (o, w) in enumerate(out)
-    ]
-
     barrier = pltpu.get_barrier_semaphore()
     for k in range(1, RING):
         pl.semaphore_signal(barrier, inc=1, device_id=xdev(k), device_id_type=MESH)
@@ -93,6 +106,25 @@
         pl.semaphore_signal(barrier, inc=1, device_id=zdev(k), device_id_type=MESH)
     for k in range(1, n_ep):
         pl.semaphore_signal(barrier, inc=1, device_id=edev(k), device_id_type=MESH)
+
+    ids_copies = [pltpu.make_async_copy(ids_hbm, ids_ref, loc_sem.at[0]),
+                  pltpu.make_async_copy(gate_hbm, gate_ref, loc_sem.at[1])]
+    tok_copy = pltpu.make_async_copy(tok_hbm, tok, loc_sem.at[2])
+    p_copies = [pltpu.make_async_copy(src, dst, loc_sem.at[3 + i])
+                for i, (src, dst) in enumerate(((p1_hbm, p1_ref), (p1t_hbm, p1t_ref), (p2_hbm, p2_ref), (p2t_hbm, p2t_ref)))]
+    for cp in ids_copies + [tok_copy] + p_copies:
+        cp.start()
+    w_loc = [
+        pltpu.make_async_copy(wg_hbm.at[0, rows(x * D4, D4), :], wgu.at[x, :, pl.ds(0, inner)], loc_sem.at[7]),
+        pltpu.make_async_copy(wu_hbm.at[0, rows(x * D4, D4), :], wgu.at[x, :, pl.ds(inner, inner)], loc_sem.at[8]),
+    ] + [
+        pltpu.make_async_copy(wd_hbm.at[0, :, cols(x * D4 + o, w)], wd.at[rows(x * inner, inner), pl.ds(o, w)], loc_sem.at[9 + q])
+        for q, (o, w) in enumerate(out)
+    ]
+
+    with scope("idswait"):
+        for cp in ids_copies:
+            cp.wait()
 
     T = tok.shape[0]
     c = lax.broadcasted_iota(jnp.int32, (slots, T), 0)
@@ -146,15 +178,19 @@
     for cp in w_loc:
         cp.start()
 
+    for cp in p_copies:
+        cp.wait()
+
     for q, (o, w) in enumerate(into):
         sl = pl.ds(o, w)
+        sp = pl.ds(o, packed(w))
         with scope("A_wait"):
             wait_bytes(xa.at[pl.ds(0, (RING - 1) * slots), sl], a_recv.at[q])
-        sb[:, sl] = dot(p1_ref[...], xa[:, sl]).astype(BF16)
+        sb[:, sp] = pack(p1_ref, xa[:, sl])
         for k in range(1, n_ep):
             dst_e = lax.rem(ep + k, n_ep)
-            send(sb.at[rows(dst_e * 16, 16), sl], rb.at[rows(ep * 16, 16), sl], B_S, b_recv.at[q], edev(k))
-        rb[rows(ep * 16, 16), sl] = sb[rows(ep * 16, 16), sl]
+            send(sb.at[rows(dst_e * 16, 16), sp], rb.at[rows(ep * 16, 16), sp], B_S, b_recv.at[q], edev(k))
+        rb[rows(ep * 16, 16), sp] = sb[rows(ep * 16, 16), sp]
 
     zm = lax.rem(zi + RING - 1, RING)
     zp = lax.rem(zi + 1, RING)
@@ -173,10 +209,11 @@
     UP, DOWN = 1, RING - 1
 
     def outset(q):
-        sl = pl.ds(*into[q])
+        o, w = into[q]
+        sp = pl.ds(o, packed(w))
         with scope("B_wait"):
-            wait_bytes(rb.at[pl.ds(0, others), sl], b_recv.at[q])
-        X[rows(zi * R, R), sl] = dot(p2_ref[...], rb[:, sl]).astype(BF16)
+            wait_bytes(rb.at[pl.ds(0, others), sp], b_recv.at[q])
+        X[rows(zi * R, R), pl.ds(o, w)] = unpack(p2_ref, rb[:, sp], w)
         zsend(q, zi, 0, zn_recv.at[q, 0], UP)
         zsend(q, zi, 1, zn_recv.at[q, 1], DOWN)
 
@@ -279,18 +316,19 @@
         y_lo = mine[:half] + rcomb[0, :, sl].astype(F32) + rdir[1, :, sl].astype(F32)
         y_hi = mine[half:] + rcomb[1, :, sl].astype(F32) + rdir[0, :, sl].astype(F32)
         y = jnp.concatenate([y_lo.astype(BF16), y_hi.astype(BF16)], axis=0)
-        sr[:, sl] = dot(p2t_ref[...], y).astype(BF16)
+        sp = pl.ds(o, packed(w))
+        sr[:, sp] = pack(p2t_ref, y)
         for k in range(1, n_ep):
             dst_e = lax.rem(ep + k, n_ep)
-            send(sr.at[rows(dst_e * 16, 16), sl], rr.at[rows(ep * 16, 16), sl], C_S, c_recv.at[q], edev(k))
-        rr[rows(ep * 16, 16), sl] = sr[rows(ep * 16, 16), sl]
+            send(sr.at[rows(dst_e * 16, 16), sp], rr.at[rows(ep * 16, 16), sp], C_S, c_recv.at[q], edev(k))
+        rr[rows(ep * 16, 16), sp] = sr[rows(ep * 16, 16), sp]
 
     def give_back(q):
         o, w = out[q]
         sl = pl.ds(o, w)
         with scope("RBw%d" % q):
-            wait_bytes(rr.at[pl.ds(0, others), sl], c_recv.at[q])
-        ts[:, sl] = dot(p1t_ref[...], rr[:, sl]).astype(BF16)
+            wait_bytes(rr.at[pl.ds(0, others), pl.ds(o, packed(w))], c_recv.at[q])
+        ts[:, sl] = unpack(p1t_ref, rr[:, pl.ds(o, packed(w))], w)
         for k in (2, 1, 3):
             dst_x = lax.rem(x + k, RING)
             send(ts.at[rows(dst_x * slots, slots), sl], ret_ref.at[:, cols(x * D4 + o, w)], E_S, d_recv, xdev(k))
@@ -314,36 +352,35 @@
         for q in range(C):
             zwait(zm_recv.at[q], q, 2)
     first(M)
-    send_down(3)
+    for q in range(3, Q):
+        send_down(q)
     for q in (1, 2):
         dwait(q)
         near(q)
         far(q)
     second(M)
     first(O)
-    dwait(3)
-    near(3)
-    far(3)
+    for q in range(3, Q):
+        dwait(q)
+        near(q)
+        far(q)
     second(O)
     hwait(M)
     for q in range(Q):
         combine(q)
     hwait(O)
-    finish(0)
-    finish(1)
-    for q in range(2, Q):
-        give_back(q - 2)
+    for q in range(Q):
         finish(q)
-    give_back(Q - 2)
-    give_back(Q - 1)
+    for q in range(Q):
+        give_back(q)
     with scope("RAw"):
         wait_bytes(ts.at[pl.ds(0, (RING - 1) * slots), :], d_recv)
     with scope("sends"):
         for group, ref in ((A_S, bs), (W_S, wgu.at[pl.ds(0, RING - 1)]),
                            (D_S, wd.at[pl.ds(0, (RING - 1) * inner), :]),
-                           (B_S, sb.at[pl.ds(0, others), :]), (Z_S, X.at[pl.ds(0, 6 * half), :]),
+                           (B_S, sb.at[pl.ds(0, others), pl.ds(0, sum(packed(w) for _, w in into))]), (Z_S, X.at[pl.ds(0, 6 * half), :]),
                            (G_S, hr), (H_S, H.at[:, :, pl.ds(0, (RING - 1) * inner)]),
-                           (R_S, X.at[pl.ds(0, 6 * half), :]), (C_S, sr.at[pl.ds(0, others), :]),
+                           (R_S, X.at[pl.ds(0, 6 * half), :]), (C_S, sr.at[pl.ds(0, others), pl.ds(0, sum(packed(w) for _, w in out))]),
                            (E_S, ts.at[pl.ds(0, (RING - 1) * slots), :])):
             wait_bytes(ref, send_sem.at[group])
 
@@ -357,15 +394,17 @@
     inner = w_down.shape[1]
     per = CAP * RING
 
-    p1 = np.zeros((n_ep * 16, R), np.float32)
-    p2 = np.zeros((R, n_ep * 16), np.float32)
+    p1 = np.zeros((1 + CAP, n_ep * 16, R), np.float32)
+    p2 = np.zeros((1 + CAP, R, n_ep * 16), np.float32)
     for e in range(n_ep):
         for s in range(RING):
             for q in range(CAP):
-                p1[e * 16 + s * CAP + q, s * slots + e * CAP + q] = 1
-        for j in range(per):
-            p2[e * per + j, e * 16 + j] = 1
-    consts = [jnp.asarray(m, BF16) for m in (p1, p1.T, p2, p2.T)]
+                j = s * CAP + q
+                p1[0, e * 16 + j, s * slots + e * CAP + q] = 1
+                p1[1 + q, e * 16 + per + s, s * slots + e * CAP + q] = 1
+                p2[0, e * per + j, e * 16 + j] = 1
+                p2[1 + q, e * per + j, e * 16 + per + s] = 1
+    consts = [jnp.asarray(m, BF16) for m in (p1, p1.transpose(0, 2, 1), p2, p2.transpose(0, 2, 1))]
 
     vm = pl.BlockSpec(memory_space=pltpu.VMEM)
     anyspec = pl.BlockSpec(memory_space=pl.ANY)
@@ -374,6 +413,8 @@
     half = R // 2
     C, Q = len(CIN), len(CHUNKS)
     scratch = [
+        V((expert_ids.shape[1], T), jnp.int32), V((expert_ids.shape[1], T), jnp.int32),
+    ] + [V(m.shape, BF16) for m in consts] + [
         V((T, width), BF16),
         V((3, slots, D4), BF16),
         V((R, D4), BF16),
@@ -395,13 +436,13 @@
         V((n_ep * 16, D4), BF16),
         V((n_ep * 16, D4), BF16),
         V((R, D4), BF16),
-        DMA((3 + Q,)), DMA((10,)), DMA(()), DMA((Q,)), DMA((C,)), DMA((C,)), DMA((C, 2)), DMA((C,)), DMA((C,)),
+        DMA((9 + Q,)), DMA((10,)), DMA(()), DMA((Q,)), DMA((C,)), DMA((C,)), DMA((C, 2)), DMA((C,)), DMA((C,)),
         DMA((4,)), DMA((4,)), DMA((Q,)), DMA((Q,)), DMA((Q,)), DMA(()),
     ]
     ret, scal = pl.pallas_call(
         kernel,
         out_shape=(pltpu.VMEM((slots, width), BF16), pltpu.VMEM((slots, T), BF16)),
-        in_specs=[vm] * 6 + [anyspec] * 4,
+        in_specs=[anyspec] * 10,
         out_specs=(vm, vm),
         scratch_shapes=scratch,
         compiler_params=pltpu.CompilerParams(collective_id=0, has_side_effects=True, vmem_limit_bytes=60 * 1024 * 1024),

time: 141 us -> 136 us (0.965)
  Pallas kernels: 139 us -> 134 us
    pallas_call x1, Pallas kernels: 139 us -> 134 us  [body(): pl.pallas_call(kernel, out_shape=(pltpu.VMEM((slots, width), BF16), pltpu...]
where the time goes in v5:
time: 136 us
  Pallas kernels  134 us (99%)
  matrix products  1.89 us (1%)
    pallas_call x1, Pallas kernels, body(): pl.pallas_call(kernel, out_shape=(pltpu.VMEM((slots, width), BF16), pltpu...  134 us

profile of v5, /device:TPU:1, one launch (start us, length us, event | category | flops | bytes accessed | tf_op | source)
XLA Modules:
  0.0 136.1 jit_solution(13100271630363008898)
XLA Ops:
  0.0 134.2 %experts.1 = (bf16[48,7168]{1,0:T(8,128)(2,1)S(1)}, bf16[48,128]{1,0:T(8,128)(2,1)S(1)}) custom-call(s32[8,128]{1,0:T(8,128)} %bitcast.4, s32[8,128]{1,0:T(8,128)} %bitcast.5, bf16[4,256,192]{2,1,0:T(8,128)(2,1)} %constant.8.clone.p1_hbm, bf16[4,192,256]{2,1,0:T(8,128)(2,1)} %constant.9.clone.p1t_hbm, bf16[4,192,256]{2,1,0:T(8,128)(2,1)} %constant.10.clone.p2_hbm, ...), custom_call_target="tpu_custom_call" | custom-call | tf_op jit(solution)/shard_map/experts/pallas_call | solution.py:442
  134.2 1.9 %convolution_convert_fusion = bf16[128,7168]{1,0:T(8,128)(2,1)} fusion(bf16[48,128]{1,0:T(8,128)(2,1)S(1)} %get-tuple-element.7, bf16[48,7168]{1,0:T(8,128)(2,1)S(1)} %get-tuple-element.8), kind=kOutput, calls=%fused_computation | convolution fusion | flops 88997888 | bytes 2535424 | tf_op jit(solution)/shard_map/dot_general | solution.py:451

commit v6 on v5

--- a/solution.py
+++ b/solution.py
@@ -48,8 +48,8 @@
 
 
 def kernel(ids_hbm, gate_hbm, p1_hbm, p1t_hbm, p2_hbm, p2t_hbm, tok_hbm, wg_hbm, wu_hbm, wd_hbm,
-           ret_ref, scal_ref,
-           ids_ref, gate_ref, p1_ref, p1t_ref, p2_ref, p2t_ref, tok, bs, xa, sb, rb, X, wgu, wd, gp, own, hr, H, pfar, pnear, pcomb, rfar, rdir, rcomb,
+           mixed_ref,
+           ret_ref, scal_ref, ids_ref, gate_ref, p1_ref, p1t_ref, p2_ref, p2t_ref, tok, bs, xa, sb, rb, X, wgu, wd, gp, own, hr, H, pfar, pnear, pcomb, rfar, rdir, rcomb,
            sr, rr, ts,
            loc_sem, send_sem, w_recv, wd_recv, a_recv, b_recv, zn_recv, zf_recv, zm_recv, g_recv,
            h_recv, rf_recv, ro_recv, c_recv, d_recv):
@@ -139,7 +139,7 @@
     before = lax.broadcasted_iota(jnp.int32, (T, T), 0) < lax.broadcasted_iota(jnp.int32, (T, T), 1)
     earlier = dot(hot.astype(BF16), jnp.where(before, 1.0, 0.0).astype(BF16))
     placing = jnp.where(earlier == slot, hot, 0.0)
-    scal_ref[...] = (placing * weight * (1.0 / 1024.0)).astype(BF16)
+    scal_ref[...] = (placing * weight * (1.0 / 1024.0)).T.astype(BF16)
     placing = placing.astype(BF16)
 
     with scope("tokwait"):
@@ -331,7 +331,7 @@
         ts[:, sl] = unpack(p1t_ref, rr[:, pl.ds(o, packed(w))], w)
         for k in (2, 1, 3):
             dst_x = lax.rem(x + k, RING)
-            send(ts.at[rows(dst_x * slots, slots), sl], ret_ref.at[:, cols(x * D4 + o, w)], E_S, d_recv, xdev(k))
+            send(ts.at[rows(dst_x * slots, slots), sl], ret_ref.at[:, cols(x * D4 + o, w)], E_S, d_recv.at[q], xdev(k))
         ret_ref[:, cols(x * D4 + o, w)] = ts[rows(x * slots, slots), sl]
 
     first(N)
@@ -373,8 +373,12 @@
         finish(q)
     for q in range(Q):
         give_back(q)
-    with scope("RAw"):
-        wait_bytes(ts.at[pl.ds(0, (RING - 1) * slots), :], d_recv)
+    for q, (o, w) in enumerate(out):
+        with scope("RAw%d" % q):
+            wait_bytes(ts.at[pl.ds(0, (RING - 1) * slots), pl.ds(o, w)], d_recv.at[q])
+        for j in range(RING):
+            sl = pl.ds(j * D4 + o, w)
+            mixed_ref[:, sl] = dot(scal_ref[...], ret_ref[:, sl]).astype(BF16)
     with scope("sends"):
         for group, ref in ((A_S, bs), (W_S, wgu.at[pl.ds(0, RING - 1)]),
                            (D_S, wd.at[pl.ds(0, (RING - 1) * inner), :]),
@@ -413,6 +417,7 @@
     half = R // 2
     C, Q = len(CIN), len(CHUNKS)
     scratch = [
+        V((slots, width), BF16), V((T, slots), BF16),
         V((expert_ids.shape[1], T), jnp.int32), V((expert_ids.shape[1], T), jnp.int32),
     ] + [V(m.shape, BF16) for m in consts] + [
         V((T, width), BF16),
@@ -437,19 +442,17 @@
         V((n_ep * 16, D4), BF16),
         V((R, D4), BF16),
         DMA((9 + Q,)), DMA((10,)), DMA(()), DMA((Q,)), DMA((C,)), DMA((C,)), DMA((C, 2)), DMA((C,)), DMA((C,)),
-        DMA((4,)), DMA((4,)), DMA((Q,)), DMA((Q,)), DMA((Q,)), DMA(()),
+        DMA((4,)), DMA((4,)), DMA((Q,)), DMA((Q,)), DMA((Q,)), DMA((Q,)),
     ]
-    ret, scal = pl.pallas_call(
+    return pl.pallas_call(
         kernel,
-        out_shape=(pltpu.VMEM((slots, width), BF16), pltpu.VMEM((slots, T), BF16)),
+        out_shape=pltpu.VMEM((T, width), BF16),
         in_specs=[anyspec] * 10,
-        out_specs=(vm, vm),
+        out_specs=vm,
         scratch_shapes=scratch,
         compiler_params=pltpu.CompilerParams(collective_id=0, has_side_effects=True, vmem_limit_bytes=60 * 1024 * 1024),
         name="experts",
     )(expert_ids.T, gate_q.T, *consts, tokens, w_gate, w_up, w_down)
-    mixed = lax.dot_general(scal, ret, (((0,), (0,)), ((), ())), preferred_element_type=F32)
-    return mixed.astype(BF16)
 
 
 def solution(mesh):

time: 136 us -> 136 us (level)
  matrix products: 1.89 us -> 0 us
    dot_general x1 -> x0, matrix products: 1.89 us -> none  [body(): lax.dot_general(scal, ret, (((0,), (0,)), ((), ())), preferred_element_ty...]
where the time goes in v6:
time: 136 us
  Pallas kernels  134 us (99%)
    pallas_call x1, Pallas kernels, body(): pl.pallas_call(kernel, out_shape=pltpu.VMEM((T, width), BF16), in_specs=[...  134 us

profile of v6, /device:TPU:1, one launch (start us, length us, event | category | flops | bytes accessed | tf_op | source)
XLA Modules:
  0.0 135.7 jit_solution(17097325479809125476)
XLA Ops:
  0.0 134.4 %experts.1 = bf16[128,7168]{1,0:T(8,128)(2,1)S(1)} custom-call(s32[8,128]{1,0:T(8,128)} %bitcast.2, s32[8,128]{1,0:T(8,128)} %bitcast.3, bf16[4,256,192]{2,1,0:T(8,128)(2,1)} %constant.8.clone.p1_hbm, bf16[4,192,256]{2,1,0:T(8,128)(2,1)} %constant.9.clone.p1t_hbm, bf16[4,192,256]{2,1,0:T(8,128)(2,1)} %constant.10.clone.p2_hbm, ...), custom_call_target="tpu_custom_call" | custom-call | tf_op jit(solution)/shard_map/experts/pallas_call | solution.py:447
  134.4 1.2 copy.12

commit v7 on v6

--- a/solution.py
+++ b/solution.py
@@ -362,12 +362,15 @@
     first(O)
     for q in range(3, Q):
         dwait(q)
-        near(q)
         far(q)
     second(O)
     hwait(M)
-    for q in range(Q):
-        combine(q)
+    combine(0)
+    combine(1)
+    for q in range(3, Q):
+        near(q)
+    combine(2)
+    combine(3)
     hwait(O)
     for q in range(Q):
         finish(q)

time: 136 us -> 135 us (level)
  no operation moved by 1% of the time
where the time goes in v7:
time: 135 us
  Pallas kernels  134 us (99%)
    pallas_call x1, Pallas kernels, body(): pl.pallas_call(kernel, out_shape=pltpu.VMEM((T, width), BF16), in_specs=[...  134 us

profile of v7, /device:TPU:1, one launch (start us, length us, event | category | flops | bytes accessed | tf_op | source)
XLA Modules:
  0.0 135.2 jit_solution(7485403331225693601)
XLA Ops:
  0.0 134.0 %experts.1 = bf16[128,7168]{1,0:T(8,128)(2,1)S(1)} custom-call(s32[8,128]{1,0:T(8,128)} %bitcast.2, s32[8,128]{1,0:T(8,128)} %bitcast.3, bf16[4,256,192]{2,1,0:T(8,128)(2,1)} %constant.8.clone.p1_hbm, bf16[4,192,256]{2,1,0:T(8,128)(2,1)} %constant.9.clone.p1t_hbm, bf16[4,192,256]{2,1,0:T(8,128)(2,1)} %constant.10.clone.p2_hbm, ...), custom_call_target="tpu_custom_call" | custom-call | tf_op jit(solution)/shard_map/experts/pallas_call | solution.py:450
  134.0 1.2 copy.12
